TPU v7x, 32 devices: a whole 2x2x4 slice. The times are simulated.
32 devices in a mesh: dp: 8 (over z, x), seq: 4 (over y, core).
Axes of the slice: x: 2, y: 2, z: 4, core: 2. Of those that a mesh axis runs over, the one named last changes fastest.
Arguments:
- queries: bfloat16 [4096, 2048], P(('dp', 'seq')), may hold values from -6 to 6
- keys: bfloat16 [4096, 2048], P(('dp', 'seq')), may hold values from -6 to 6
- values: bfloat16 [4096, 2048], P(('dp', 'seq')), may hold values from -6 to 6
- q_gain: float32 [2048], replicated, may hold values from 0.25 to 1.75
- k_gain: float32 [2048], replicated, may hold values from 0.25 to 1.75
- out_grad: bfloat16 [4096, 2048], P(('dp', 'seq')), may hold values from -16 to 16
- segments: int32 [8, 512], P('dp'), may hold values from 0 to 3, never falling along the last dimension, each value on 1 to 256 neighbouring positions
- visible: int32 [8, 512], P('dp'), may hold values 0 or 1
Outputs:
- attn_out: bfloat16 [4096, 2048], P(('dp', 'seq'))
- query_grad: bfloat16 [4096, 2048], P(('dp', 'seq'))
- key_grad: bfloat16 [4096, 2048], P(('dp', 'seq'))
- value_grad: bfloat16 [4096, 2048], P(('dp', 'seq'))
- q_gain_grad: float32 [2048], replicated
- k_gain_grad: float32 [2048], replicated
Inputs may be any that keep to these rules, and one draw needn't show every extreme that they name: `segments`: along each packed sequence the clip numbers never fall; each of the 4 clips holds 1 to 256 slots.
All inputs are finite; a program needn't handle non-finite values. No bound on the sum of `visible` on one device may be relied on, other than what follows from the above.
Results may differ from a plain program's by a relative error of at most 0.012.
The roundings to bfloat16 on the way count: a program that leaves them out, or rounds other values in their place, can miss the bound.
Values may be sent and summed in bfloat16 or wider, within the bound.
No kernel may reach another device: no remote copies, remote signals or barrier semaphores. Data moves between devices by JAX's collectives and lax.ppermute only.
A program may use at most 64 MiB of HBM per device.

v0:
```python
import jax
import jax.numpy as jnp
from jax import lax
from jax.sharding import PartitionSpec as P

D_HEAD = 128


epsilon = 1e-06


def normalize(raw_rows, gain_vec):
    raw_f32 = raw_rows.astype(jnp.float32)
    inv_rms = lax.rsqrt(jnp.mean(raw_f32 * raw_f32, axis=-1, keepdims=True) + epsilon)
    return ((raw_f32 * inv_rms * gain_vec).astype(jnp.bfloat16), inv_rms)


def norm_back(raw_rows, inv_rms, gain_vec, grad_norm):
    raw_f32 = raw_rows.astype(jnp.float32)
    grad_f32 = grad_norm.astype(jnp.float32)
    scaled_grad = gain_vec * grad_f32
    mean_term = jnp.mean(scaled_grad * raw_f32, axis=-1, keepdims=True)
    grad_raw = inv_rms * scaled_grad - raw_f32 * inv_rms**3 * mean_term
    return (grad_raw.astype(jnp.bfloat16), jnp.sum(grad_f32 * raw_f32 * inv_rms, axis=0))


def attend(q_norm, k_norm, val_rows, grad_rows, seg_row, vis_row, keep_out):
    seq_rows, feature_count = q_norm.shape
    head_count = feature_count // D_HEAD
    score_scale = D_HEAD ** (-0.5)
    block_rows = 512
    block_count = seq_rows // block_rows
    k_three = k_norm.reshape(seq_rows, head_count, D_HEAD)
    v_three = val_rows.reshape(seq_rows, head_count, D_HEAD)
    positions = jnp.arange(seq_rows, dtype=jnp.int32)
    key_open = vis_row == 1

    def one_block(totals, block_index):
        block_start = block_index * block_rows
        q_block = lax.dynamic_slice_in_dim(q_norm, block_start, block_rows, 0).reshape(
            block_rows, head_count, D_HEAD
        )
        seg_block = lax.dynamic_slice_in_dim(seg_row, block_start, block_rows, 0)
        pos_block = block_start + jnp.arange(block_rows, dtype=jnp.int32)
        allowed = (seg_block[:, None] == seg_row[None, :]) & (
            key_open[None, :] | (pos_block[:, None] == positions[None, :])
        )
        scores = (
            jnp.einsum("shd,thd->hst", q_block, k_three, preferred_element_type=jnp.float32)
            * score_scale
        )
        scores = jnp.where(allowed[None], scores, -1e30)
        row_max = jnp.max(scores, axis=-1, keepdims=True)
        weights = jnp.exp(scores - row_max)
        attn_prob = weights / jnp.sum(weights, axis=-1, keepdims=True)
        prob_half = attn_prob.astype(jnp.bfloat16)
        block_out = jnp.zeros((block_rows, feature_count), jnp.bfloat16)
        if keep_out:
            block_out = (
                jnp.einsum("hst,thd->shd", prob_half, v_three, preferred_element_type=jnp.float32)
                .reshape(block_rows, feature_count)
                .astype(jnp.bfloat16)
            )
        if grad_rows is None:
            return (totals, (block_out, block_out))
        grad_block = lax.dynamic_slice_in_dim(grad_rows, block_start, block_rows, 0).reshape(
            block_rows, head_count, D_HEAD
        )
        dprob = jnp.einsum("shd,thd->hst", grad_block, v_three, preferred_element_type=jnp.float32)
        value_add = jnp.einsum(
            "hst,shd->thd", prob_half, grad_block, preferred_element_type=jnp.float32
        )
        row_dot = jnp.sum(attn_prob * dprob, axis=-1, keepdims=True)
        score_grad = (attn_prob * (dprob - row_dot) * score_scale).astype(jnp.bfloat16)
        q_grad = (
            jnp.einsum("hst,thd->shd", score_grad, k_three, preferred_element_type=jnp.float32)
            .reshape(block_rows, feature_count)
            .astype(jnp.bfloat16)
        )
        key_add = jnp.einsum(
            "hst,shd->thd", score_grad, q_block, preferred_element_type=jnp.float32
        )
        return ((totals[0] + key_add, totals[1] + value_add), (block_out, q_grad))

    empty = jnp.zeros((seq_rows, head_count, D_HEAD), jnp.float32)
    totals, stacked = lax.scan(one_block, (empty, empty), jnp.arange(block_count, dtype=jnp.int32))
    attn_out = stacked[0].reshape(seq_rows, feature_count)
    if grad_rows is None:
        return attn_out
    q_grad = stacked[1].reshape(seq_rows, feature_count)
    k_grad = totals[0].reshape(seq_rows, feature_count).astype(jnp.bfloat16)
    v_grad = totals[1].reshape(seq_rows, feature_count).astype(jnp.bfloat16)
    return (attn_out, q_grad, k_grad, v_grad)


def per_device(queries, keys, values, q_gain, k_gain, out_grad, segments, visible):
    q_norm, q_inv = normalize(queries, q_gain)
    k_norm, k_inv = normalize(keys, k_gain)
    seg_row = segments[0]
    vis_row = visible[0]
    query_heads, key_heads, value_heads = (
        lax.all_to_all(q_norm, "seq", split_axis=1, concat_axis=0, tiled=True),
        lax.all_to_all(k_norm, "seq", split_axis=1, concat_axis=0, tiled=True),
        lax.all_to_all(values, "seq", split_axis=1, concat_axis=0, tiled=True),
    )
    out_part = attend(query_heads, key_heads, value_heads, None, seg_row, vis_row, True)
    attn_out = lax.all_to_all(out_part, "seq", split_axis=0, concat_axis=1, tiled=True)
    grad_heads = lax.all_to_all(out_grad, "seq", split_axis=1, concat_axis=0, tiled=True)
    unused_out, q_part, k_part, v_part = attend(
        query_heads, key_heads, value_heads, grad_heads, seg_row, vis_row, False
    )
    q_grad, k_grad, value_grad = (
        lax.all_to_all(q_part, "seq", split_axis=0, concat_axis=1, tiled=True),
        lax.all_to_all(k_part, "seq", split_axis=0, concat_axis=1, tiled=True),
        lax.all_to_all(v_part, "seq", split_axis=0, concat_axis=1, tiled=True),
    )
    query_grad, q_gain_part = norm_back(queries, q_inv, q_gain, q_grad)
    key_grad, k_gain_part = norm_back(keys, k_inv, k_gain, k_grad)
    q_gain_grad, k_gain_grad = lax.psum((q_gain_part, k_gain_part), ("dp", "seq"))
    return (attn_out, query_grad, key_grad, value_grad, q_gain_grad, k_gain_grad)


def solution(mesh):
    return jax.shard_map(
        per_device,
        mesh=mesh,
        in_specs=(
            P(("dp", "seq"), None),
            P(("dp", "seq"), None),
            P(("dp", "seq"), None),
            P(),
            P(),
            P(("dp", "seq"), None),
            P("dp", None),
            P("dp", None),
        ),
        out_specs=(
            P(("dp", "seq"), None),
            P(("dp", "seq"), None),
            P(("dp", "seq"), None),
            P(("dp", "seq"), None),
            P(),
            P(),
        ),
        check_vma=False,
    )
```

profile of v0, /device:TPU:0, one launch (start us, length us, event | category | flops | bytes accessed | tf_op | source)
XLA Modules:
  0.0 164.4 jit_solution(12461290162924541765)
XLA Ops:
  0.7 1.3 fusion.31
  4.1 4.3 %all-to-all-start = ((bf16[128,4,512]{2,0,1:T(8,128)(2,1)}), bf16[128,4,512]{2,0,1:T(8,128)(2,1)S(1)}, u32[]{:S(2)}, u32[]{:S(2)}) async-start(bf16[128,4,512]{2,0,1:T(8,128)(2,1)} %bitcast.48), calls=%async_computation | async-start | bytes 1048576 | tf_op jit(solution)/shard_map/all_to_all | solution.py:102
  10.7 6.5 %all-to-all-done = bf16[128,4,512]{2,0,1:T(8,128)(2,1)S(1)} async-done(((bf16[128,4,512]{2,0,1:T(8,128)(2,1)}), bf16[128,4,512]{2,0,1:T(8,128)(2,1)S(1)}, u32[]{:S(2)}, u32[]{:S(2)}) %all-to-all-start) | async-done | bytes 524320 | tf_op jit(solution)/shard_map/all_to_all | solution.py:102
  17.2 3.5 %all-to-all-start.1 = ((bf16[128,4,512]{2,0,1:T(8,128)(2,1)}), bf16[128,4,512]{2,0,1:T(8,128)(2,1)S(1)}, u32[]{:S(2)}, u32[]{:S(2)}) async-start(bf16[128,4,512]{2,0,1:T(8,128)(2,1)} %bitcast.47), calls=%async_computation.1 | async-start | bytes 1048576 | tf_op jit(solution)/shard_map/all_to_all | solution.py:103
  21.5 7.9 %all-to-all-done.1 = bf16[128,4,512]{2,0,1:T(8,128)(2,1)S(1)} async-done(((bf16[128,4,512]{2,0,1:T(8,128)(2,1)}), bf16[128,4,512]{2,0,1:T(8,128)(2,1)S(1)}, u32[]{:S(2)}, u32[]{:S(2)}) %all-to-all-start.1) | async-done | bytes 524320 | tf_op jit(solution)/shard_map/all_to_all | solution.py:103
  29.4 3.5 %all-to-all-start.2 = ((bf16[128,4,512]{2,0,1:T(8,128)(2,1)}), bf16[128,4,512]{2,0,1:T(8,128)(2,1)S(1)}, u32[]{:S(2)}, u32[]{:S(2)}) async-start(bf16[128,4,512]{2,0,1:T(8,128)(2,1)} %bitcast.46), calls=%async_computation.2 | async-start | bytes 1048576 | tf_op jit(solution)/shard_map/all_to_all | solution.py:104
  33.8 7.9 %all-to-all-done.2 = bf16[128,4,512]{2,0,1:T(8,128)(2,1)S(1)} async-done(((bf16[128,4,512]{2,0,1:T(8,128)(2,1)}), bf16[128,4,512]{2,0,1:T(8,128)(2,1)S(1)}, u32[]{:S(2)}, u32[]{:S(2)}) %all-to-all-start.2) | async-done | bytes 524320 | tf_op jit(solution)/shard_map/all_to_all | solution.py:104
  41.7 3.5 %all-to-all-start.4 = ((bf16[128,4,512]{2,0,1:T(8,128)(2,1)}), bf16[128,4,512]{2,0,1:T(8,128)(2,1)S(1)}, u32[]{:S(2)}, u32[]{:S(2)}) async-start(bf16[128,4,512]{2,0,1:T(8,128)(2,1)} %bitcast.45), calls=%async_computation.4 | async-start | bytes 1048576 | tf_op jit(solution)/shard_map/all_to_all | solution.py:108
  47.3 6.6 %all-to-all-done.4 = bf16[128,4,512]{2,0,1:T(8,128)(2,1)S(1)} async-done(((bf16[128,4,512]{2,0,1:T(8,128)(2,1)}), bf16[128,4,512]{2,0,1:T(8,128)(2,1)S(1)}, u32[]{:S(2)}, u32[]{:S(2)}) %all-to-all-start.4) | async-done | bytes 524320 | tf_op jit(solution)/shard_map/all_to_all | solution.py:108
  54.1 4.7 %fusion.66 = (f32[4,512]{1,0:T(4,128)S(1)}, f32[4,512,512]{1,2,0:T(8,128)}) fusion(pred[512,512]{0,1:T(8,128)(4,1)S(1)} %fusion.52, bf16[512,4,128]{0,2,1:T(8,128)(2,1)} %copy.79, bf16[512,4,128]{0,2,1:T(8,128)(2,1)S(1)} %copy.75), kind=kOutput, calls=%fused_computation.80 | convolution fusion | flops 272630272 | bytes 5513216 | tf_op jit(solution)/shard_map/while/body/eval_jaxpr/sub | solution.py:54
  58.7 2.9 %fusion.30 = bf16[512,4,128]{2,0,1:T(8,128)(2,1)S(1)} fusion(bf16[512,4,128]{2,1,0:T(4,128)(2,1)S(1)} %reshape.192, f32[4,512,512]{1,2,0:T(8,128)} %get-tuple-element.92, f32[4,512]{1,0:T(4,128)S(1)} %get-tuple-element.91), kind=kOutput, calls=%fused_computation.33 | convolution fusion | flops 270794752 | bytes 5251072 | tf_op jit(solution)/shard_map/while/body/eval_jaxpr/hst,shd->thd/dot_general | solution.py:70
  63.1 3.5 %all-to-all-start.7 = ((bf16[4,128,512]{2,1,0:T(8,128)(2,1)}), bf16[4,128,512]{2,1,0:T(8,128)(2,1)S(1)}, u32[]{:S(2)}, u32[]{:S(2)}) async-start(bf16[4,128,512]{2,1,0:T(8,128)(2,1)} %convert_element_type.117), calls=%async_computation.7 | async-start | bytes 1048576 | tf_op jit(solution)/shard_map/all_to_all | solution.py:115
  66.5 3.1 %fusion.29 = bf16[512,4,128]{2,0,1:T(8,128)(2,1)S(1)} fusion(bf16[512,4,128]{2,1,0:T(4,128)(2,1)S(1)} %reshape.191, f32[4,512,512]{1,2,0:T(8,128)} %get-tuple-element.92, f32[4,512]{1,0:T(4,128)S(1)} %get-tuple-element.91), kind=kOutput, calls=%fused_computation.32 | convolution fusion | flops 270794752 | bytes 5251072 | tf_op jit(solution)/shard_map/while/body/eval_jaxpr/hst,thd->shd/dot_general | solution.py:60
  71.1 4.3 %all-to-all-done.7 = bf16[4,128,512]{2,1,0:T(8,128)(2,1)S(1)} async-done(((bf16[4,128,512]{2,1,0:T(8,128)(2,1)}), bf16[4,128,512]{2,1,0:T(8,128)(2,1)S(1)}, u32[]{:S(2)}, u32[]{:S(2)}) %all-to-all-start.7) | async-done | bytes 524320 | tf_op jit(solution)/shard_map/all_to_all | solution.py:115
  75.3 3.5 %all-to-all-start.3 = ((bf16[4,128,512]{2,1,0:T(8,128)(2,1)}), bf16[4,128,512]{2,1,0:T(8,128)(2,1)S(1)}, u32[]{:S(2)}, u32[]{:S(2)}) async-start(bf16[4,128,512]{2,1,0:T(8,128)(2,1)} %convert_element_type.99), calls=%async_computation.3 | async-start | bytes 1048576 | tf_op jit(solution)/shard_map/all_to_all | solution.py:107
  78.8 2.7 %fusion.54 = f32[4,512,512]{1,2,0:T(8,128)} fusion(bf16[512,4,128]{2,1,0:T(4,128)(2,1)S(1)} %reshape.192, bf16[512,4,128]{2,1,0:T(4,128)(2,1)S(1)} %reshape.191), kind=kOutput, calls=%fused_computation.62 | convolution fusion | flops 268435456 | bytes 5242880 | tf_op jit(solution)/shard_map/while/body/eval_jaxpr/shd,thd->hst/dot_general | solution.py:69
  81.5 7.6 %fusion.23 = bf16[512,4,128]{0,2,1:T(8,128)(2,1)S(1)} fusion(bf16[512,4,128]{0,2,1:T(8,128)(2,1)} %copy.79, f32[4,512,512]{1,2,0:T(8,128)} %fusion.54, f32[4,512,512]{1,2,0:T(8,128)} %get-tuple-element.92, f32[4,512]{1,0:T(4,128)S(1)} %get-tuple-element.91), kind=kOutput, calls=%fused_computation.30 | convolution fusion | flops 276040192 | bytes 9445376 | tf_op jit(solution)/shard_map/while/body/eval_jaxpr/hst,shd->thd/dot_general | solution.py:80
  90.1 3.5 %all-to-all-start.6 = ((bf16[4,128,512]{1,2,0:T(8,128)(2,1)}), bf16[4,128,512]{1,2,0:T(8,128)(2,1)S(1)}, u32[]{:S(2)}, u32[]{:S(2)}) async-start(bf16[4,128,512]{1,2,0:T(8,128)(2,1)} %copy.81), calls=%async_computation.6 | async-start | bytes 1048576 | tf_op jit(solution)/shard_map/all_to_all | solution.py:114
  93.6 8.5 %fusion.26 = bf16[512,4,128]{0,2,1:T(8,128)(2,1)} fusion(bf16[512,4,128]{0,2,1:T(8,128)(2,1)S(1)} %copy.75, f32[4,512,512]{1,2,0:T(8,128)} %fusion.54, f32[4,512,512]{1,2,0:T(8,128)} %get-tuple-element.92, f32[4,512]{1,0:T(4,128)S(1)} %get-tuple-element.91), kind=kOutput, calls=%fused_computation.31 | convolution fusion | flops 276040192 | bytes 9445376 | tf_op jit(solution)/shard_map/while/body/eval_jaxpr/hst,thd->shd/dot_general | solution.py:76
  104.2 4.3 %all-to-all-start.5 = ((bf16[4,128,512]{1,2,0:T(8,128)(2,1)}), bf16[4,128,512]{1,2,0:T(8,128)(2,1)}, u32[]{:S(2)}, u32[]{:S(2)}) async-start(bf16[4,128,512]{1,2,0:T(8,128)(2,1)} %copy.77), calls=%async_computation.5 | async-start | bytes 1048576 | tf_op jit(solution)/shard_map/all_to_all | solution.py:113
  111.5 5.8 %all-to-all-done.5 = bf16[4,128,512]{1,2,0:T(8,128)(2,1)} async-done(((bf16[4,128,512]{1,2,0:T(8,128)(2,1)}), bf16[4,128,512]{1,2,0:T(8,128)(2,1)}, u32[]{:S(2)}, u32[]{:S(2)}) %all-to-all-start.5) | async-done | bytes 524320 | tf_op jit(solution)/shard_map/all_to_all | solution.py:113
  117.3 2.1 %convert_element_type.120 = f32[4,128,512]{1,2,0:T(8,128)} convert(bf16[4,128,512]{1,2,0:T(8,128)(2,1)} %all-to-all-done.5) | non-fusion elementwise | flops 262144 | bytes 1572864 | tf_op jit(solution)/shard_map/convert_element_type | solution.py:20
  119.4 1.6 copy.78
  121.7 40.3 %all-reduce = (f32[2048]{0:T(1024)}, f32[2048]{0:T(1024)}) all-reduce(f32[2048]{0:T(1024)S(1)} %get-tuple-element.71, f32[2048]{0:T(1024)S(1)} %get-tuple-element.94), channel_id=1, replica_groups=mesh['dp'=8,'seq'=4] {'dp','seq'}, use_global_device_ids=true, to_apply=%region_8.9 | all-reduce | flops 4096 | bytes 32768 | tf_op jit(solution)/shard_map/psum | solution.py:119
  (54 shorter events, 20.2 us)
Async XLA Ops:
  0.6 9.0 %copy-start.1 = (bf16[128,2048]{1,0:T(8,128)(2,1)S(1)}, bf16[128,2048]{1,0:T(8,128)(2,1)}, u32[]{:S(2)}) copy-start(bf16[128,2048]{1,0:T(8,128)(2,1)} %param.9) | copy-start | bytes 1572868
  0.6 9.0 %copy-start.5 = (f32[2048]{0:T(1024)S(1)}, f32[2048]{0:T(1024)}, u32[]{:S(2)}) copy-start(f32[2048]{0:T(1024)} %param.12) | copy-start | bytes 24580
  0.7 20.0 %copy-start.2 = (bf16[128,2048]{1,0:T(8,128)(2,1)S(1)}, bf16[128,2048]{1,0:T(8,128)(2,1)}, u32[]{:S(2)}) copy-start(bf16[128,2048]{1,0:T(8,128)(2,1)} %param.10) | copy-start | bytes 1572868
  3.2 29.7 %copy-start.3 = (bf16[128,2048]{1,0:T(8,128)(2,1)S(1)}, bf16[128,2048]{1,0:T(8,128)(2,1)}, u32[]{:S(2)}) copy-start(bf16[128,2048]{1,0:T(8,128)(2,1)} %param.13) | copy-start | bytes 1572868
  4.1 13.1 %all-to-all-start = ((bf16[128,4,512]{2,0,1:T(8,128)(2,1)}), bf16[128,4,512]{2,0,1:T(8,128)(2,1)S(1)}, u32[]{:S(2)}, u32[]{:S(2)}) async-start(bf16[128,4,512]{2,0,1:T(8,128)(2,1)} %bitcast.48), calls=%async_computation | async-start | bytes 1048576 | tf_op jit(solution)/shard_map/all_to_all | solution.py:102
  8.3 36.8 %copy-start.7 = (s32[1,512]{1,0:T(1,128)S(1)}, s32[1,512]{1,0:T(1,128)}, u32[]{:S(2)}) copy-start(s32[1,512]{1,0:T(1,128)} %param.15) | copy-start | bytes 6148
  8.3 36.8 %copy-start.6 = (s32[1,512]{1,0:T(1,128)S(1)}, s32[1,512]{1,0:T(1,128)}, u32[]{:S(2)}) copy-start(s32[1,512]{1,0:T(1,128)} %param.14) | copy-start | bytes 6148
  17.2 12.3 %all-to-all-start.1 = ((bf16[128,4,512]{2,0,1:T(8,128)(2,1)}), bf16[128,4,512]{2,0,1:T(8,128)(2,1)S(1)}, u32[]{:S(2)}, u32[]{:S(2)}) async-start(bf16[128,4,512]{2,0,1:T(8,128)(2,1)} %bitcast.47), calls=%async_computation.1 | async-start | bytes 1048576 | tf_op jit(solution)/shard_map/all_to_all | solution.py:103
  29.4 12.3 %all-to-all-start.2 = ((bf16[128,4,512]{2,0,1:T(8,128)(2,1)}), bf16[128,4,512]{2,0,1:T(8,128)(2,1)S(1)}, u32[]{:S(2)}, u32[]{:S(2)}) async-start(bf16[128,4,512]{2,0,1:T(8,128)(2,1)} %bitcast.46), calls=%async_computation.2 | async-start | bytes 1048576 | tf_op jit(solution)/shard_map/all_to_all | solution.py:104
  41.7 12.3 %all-to-all-start.4 = ((bf16[128,4,512]{2,0,1:T(8,128)(2,1)}), bf16[128,4,512]{2,0,1:T(8,128)(2,1)S(1)}, u32[]{:S(2)}, u32[]{:S(2)}) async-start(bf16[128,4,512]{2,0,1:T(8,128)(2,1)} %bitcast.45), calls=%async_computation.4 | async-start | bytes 1048576 | tf_op jit(solution)/shard_map/all_to_all | solution.py:108
  63.1 12.3 %all-to-all-start.7 = ((bf16[4,128,512]{2,1,0:T(8,128)(2,1)}), bf16[4,128,512]{2,1,0:T(8,128)(2,1)S(1)}, u32[]{:S(2)}, u32[]{:S(2)}) async-start(bf16[4,128,512]{2,1,0:T(8,128)(2,1)} %convert_element_type.117), calls=%async_computation.7 | async-start | bytes 1048576 | tf_op jit(solution)/shard_map/all_to_all | solution.py:115
  75.3 14.8 %all-to-all-start.3 = ((bf16[4,128,512]{2,1,0:T(8,128)(2,1)}), bf16[4,128,512]{2,1,0:T(8,128)(2,1)S(1)}, u32[]{:S(2)}, u32[]{:S(2)}) async-start(bf16[4,128,512]{2,1,0:T(8,128)(2,1)} %convert_element_type.99), calls=%async_computation.3 | async-start | bytes 1048576 | tf_op jit(solution)/shard_map/all_to_all | solution.py:107
  90.1 14.0 %all-to-all-start.6 = ((bf16[4,128,512]{1,2,0:T(8,128)(2,1)}), bf16[4,128,512]{1,2,0:T(8,128)(2,1)S(1)}, u32[]{:S(2)}, u32[]{:S(2)}) async-start(bf16[4,128,512]{1,2,0:T(8,128)(2,1)} %copy.81), calls=%async_computation.6 | async-start | bytes 1048576 | tf_op jit(solution)/shard_map/all_to_all | solution.py:114
  104.2 13.2 %all-to-all-start.5 = ((bf16[4,128,512]{1,2,0:T(8,128)(2,1)}), bf16[4,128,512]{1,2,0:T(8,128)(2,1)}, u32[]{:S(2)}, u32[]{:S(2)}) async-start(bf16[4,128,512]{1,2,0:T(8,128)(2,1)} %copy.77), calls=%async_computation.5 | async-start | bytes 1048576 | tf_op jit(solution)/shard_map/all_to_all | solution.py:113
  110.0 10.9 %copy-start = (bf16[128,2048]{1,0:T(8,128)(2,1)S(1)}, bf16[128,2048]{1,0:T(8,128)(2,1)}, u32[]{:S(2)}) copy-start(bf16[128,2048]{1,0:T(8,128)(2,1)} %param.8) | copy-start | bytes 1572868
  110.1 10.9 %copy-start.4 = (f32[2048]{0:T(1024)S(1)}, f32[2048]{0:T(1024)}, u32[]{:S(2)}) copy-start(f32[2048]{0:T(1024)} %param.11) | copy-start | bytes 24580
where the time goes:
time: 165 us; the launch traced here: 164 us
  blocking collectives  40.3 us (24%)
  waiting for transfers between devices  39.1 us (24%)
  matrix products  29.5 us (18%)
  starting transfers between devices  29.4 us (18%)
  local copies, waits for them, and re-layouts  15.6 us (9%)
  other arithmetic  9.54 us (6%)
    psum x1, blocking collectives, per_device(): lax.psum((q_gain_part, k_gain_part), ('dp', 'seq'))  40.3 us
    dot_general x1, matrix products, one_block(): jnp.einsum('hst,thd->shd', score_grad, k_three, preferred_element_type=jn...  8.53 us
    all_to_all x1, waiting for transfers between devices, per_device(): lax.all_to_all(k_norm, 'seq', split_axis=1, concat_axis=0, tiled=True)  7.93 us
    all_to_all x1, waiting for transfers between devices, per_device(): lax.all_to_all(values, 'seq', split_axis=1, concat_axis=0, tiled=True)  7.93 us
    dot_general x1, matrix products, one_block(): jnp.einsum('hst,shd->thd', score_grad, q_block, preferred_element_type=jn...  7.62 us
    all_to_all x1, waiting for transfers between devices, per_device(): lax.all_to_all(out_grad, 'seq', split_axis=1, concat_axis=0, tiled=True)  6.63 us
    all_to_all x1, waiting for transfers between devices, per_device(): lax.all_to_all(q_norm, 'seq', split_axis=1, concat_axis=0, tiled=True)  6.49 us
    all_to_all x1, waiting for transfers between devices, per_device(): lax.all_to_all(q_part, 'seq', split_axis=0, concat_axis=1, tiled=True)  5.84 us
  transfers between devices with their start and end apart: 8, of which 6 were waited for; matrix products, arithmetic and copies ran while one was open for 22% of the time, Pallas kernels for 0%

commit v1 on v0

v1 whole, which is shorter than its diff:
```python
import functools

import jax
import jax.numpy as jnp
from jax import lax
from jax.experimental import pallas as pl
from jax.experimental.pallas import tpu as pltpu
from jax.sharding import PartitionSpec as P


D_HEAD = 128
UNIT = 16
CORES = 2
EPSILON = 1e-06
NEG = -1e30
PREPARE_STEPS = 2
LOCAL_GROUP = 4
CROSS_GROUPS = (2, 1)
FIRST_UNITS = 27


def normalize(raw_rows, gain_vec):
    raw_f32 = raw_rows.astype(jnp.float32)
    inv_rms = lax.rsqrt(jnp.mean(raw_f32 * raw_f32, axis=-1, keepdims=True) + EPSILON)
    return ((raw_f32 * inv_rms * gain_vec).astype(jnp.bfloat16), inv_rms)


def norm_back(raw_rows, inv_rms, gain_vec, grad_norm):
    raw_f32 = raw_rows.astype(jnp.float32)
    grad_f32 = grad_norm.astype(jnp.float32)
    scaled_grad = gain_vec * grad_f32
    mean_term = jnp.mean(scaled_grad * raw_f32, axis=-1, keepdims=True)
    grad_raw = inv_rms * scaled_grad - raw_f32 * inv_rms**3 * mean_term
    return (grad_raw.astype(jnp.bfloat16), jnp.sum(grad_f32 * raw_f32 * inv_rms, axis=0))


def attend(q_norm, k_norm, val_rows, grad_rows, seg_row, vis_row):
    seq_rows, feature_count = q_norm.shape
    heads = feature_count // D_HEAD
    scale = D_HEAD ** (-0.5)
    positions = jnp.arange(seq_rows, dtype=jnp.int32)
    allowed = (seg_row[:, None] == seg_row[None, :]) & (
        (vis_row[None, :] == 1) | (positions[:, None] == positions[None, :])
    )
    f32 = jnp.float32
    q, k, v, g = (
        x.reshape(seq_rows, heads, D_HEAD) for x in (q_norm, k_norm, val_rows, grad_rows)
    )
    scores = jnp.einsum("shd,thd->hst", q, k, preferred_element_type=f32) * scale
    scores = jnp.where(allowed[None], scores, NEG)
    weights = jnp.exp(scores - jnp.max(scores, axis=-1, keepdims=True))
    prob = weights / jnp.sum(weights, axis=-1, keepdims=True)
    half = prob.astype(jnp.bfloat16)
    out = jnp.einsum("hst,thd->shd", half, v, preferred_element_type=f32)
    dprob = jnp.einsum("shd,thd->hst", g, v, preferred_element_type=f32)
    v_grad = jnp.einsum("hst,shd->thd", half, g, preferred_element_type=f32)
    row_dot = jnp.sum(prob * dprob, axis=-1, keepdims=True)
    score_grad = (prob * (dprob - row_dot) * scale).astype(jnp.bfloat16)
    q_grad = jnp.einsum("hst,thd->shd", score_grad, k, preferred_element_type=f32)
    k_grad = jnp.einsum("hst,shd->thd", score_grad, q, preferred_element_type=f32)
    return tuple(
        x.reshape(seq_rows, feature_count).astype(jnp.bfloat16)
        for x in (out, q_grad, k_grad, v_grad)
    )


def per_device_any(queries, keys, values, q_gain, k_gain, out_grad, segments, visible):
    q_norm, q_inv = normalize(queries, q_gain)
    k_norm, k_inv = normalize(keys, k_gain)
    gather = functools.partial(
        lax.all_to_all, axis_name="seq", split_axis=1, concat_axis=0, tiled=True
    )
    spread = functools.partial(
        lax.all_to_all, axis_name="seq", split_axis=0, concat_axis=1, tiled=True
    )
    parts = attend(
        *(gather(x) for x in (q_norm, k_norm, values, out_grad)), segments[0], visible[0]
    )
    attn_out, q_grad, k_grad, value_grad = (spread(x) for x in parts)
    query_grad, q_gain_part = norm_back(queries, q_inv, q_gain, q_grad)
    key_grad, k_gain_part = norm_back(keys, k_inv, k_gain, k_grad)
    q_gain_grad, k_gain_grad = lax.psum((q_gain_part, k_gain_part), ("dp", "seq"))
    return (attn_out, query_grad, key_grad, value_grad, q_gain_grad, k_gain_grad)


def units_needed(blocks, heads):
    worst = 0
    for ka in range(1, blocks + 1):
        for kb in range(1, blocks + 2 - ka):
            worst = max(worst, min(max(ka * (heads - h), kb * h) for h in range(heads + 1)))
    return worst


def dot(x, y, dims):
    return lax.dot_general(x, y, (dims, ((), ())), preferred_element_type=jnp.float32)


NT = ((1,), (1,))
NN = ((1,), (0,))
TN = ((0,), (0,))
LOG2_E = 1.4426950408889634


def attention(q, k, v, g, bias):
    scale = D_HEAD ** (-0.5)
    scores = dot(k, q, NT) * (scale * LOG2_E) + bias
    weights = jnp.exp2(scores - jnp.max(scores, axis=0, keepdims=True))
    prob = weights * (1.0 / jnp.sum(weights, axis=0, keepdims=True))
    half = prob.astype(jnp.bfloat16)
    out = dot(half, v, TN)
    dprob = dot(v, g, NT)
    v_grad = dot(half, g, NN)
    row_dot = jnp.sum(prob * dprob, axis=0, keepdims=True)
    score_grad = (prob * scale * (dprob - row_dot)).astype(jnp.bfloat16)
    q_grad = dot(score_grad, k, TN)
    k_grad = dot(score_grad, q, NN)
    return tuple(x.astype(jnp.bfloat16) for x in (out, q_grad, k_grad, v_grad))


def own_side(plan):
    first = plan[0] == 0
    heads = plan[8]
    j0 = jnp.where(first, plan[6], 0)
    j1 = jnp.where(first, heads, plan[6])
    k_own = jnp.where(first, plan[4], plan[5])
    row0 = jnp.where(first, plan[9] - UNIT * plan[4], 0)
    return j0, j1, k_own, row0


def prepare_kernel(rows, heads, budget, steps, q_hbm, k_hbm, v_hbm, g_hbm, qg_hbm, kg_hbm, seg_hbm,
                   mine_ref, theirs_ref, inv_ref, plan_ref, q_ref, k_ref, qg_ref, kg_ref, seg_ref,
                   sems, head_sems):
    core = lax.rem(lax.axis_index("seq"), CORES)
    part = rows // steps

    def fetch(n, source, target):
        copy = pltpu.make_async_copy(source, target, sems.at[n])
        copy.start()
        return copy

    seg_copy = fetch(0, seg_hbm, seg_ref)
    gain_copies = [fetch(1, qg_hbm, qg_ref), fetch(2, kg_hbm, kg_ref)]
    raw_copies = []
    for n, (source, target) in enumerate(((q_hbm, q_ref), (k_hbm, k_ref))):
        for step in range(steps):
            here = pl.ds(step * part, part)
            raw_copies.append(fetch(3 + n * steps + step, source.at[here], target.at[here]))
    head_copies = []
    for n, source in ((2, v_hbm), (3, g_hbm)):
        for half, target in ((core, mine_ref), (1 - core, theirs_ref)):
            for j in range(heads):
                col = pl.ds(pl.multiple_of((half * heads + j) * D_HEAD, D_HEAD), D_HEAD)
                copy = pltpu.make_async_copy(
                    source.at[:, col], target.at[n, j], head_sems.at[len(head_copies)]
                )
                copy.start()
                head_copies.append(copy)

    seg_copy.wait()
    seg = seg_ref[...].astype(jnp.float32)
    chip_rows = seg.shape[1] // 2
    at = lax.broadcasted_iota(jnp.int32, seg.shape, 1)
    edge = jnp.sum(jnp.where(at == chip_rows - 1, seg, 0.0))
    beyond = jnp.sum(jnp.where(at == chip_rows, seg, 0.0))
    crosses = edge == beyond
    same = seg == edge
    a = jnp.sum(jnp.where(same & (at < chip_rows), 1.0, 0.0)).astype(jnp.int32)
    b = jnp.sum(jnp.where(same & (at >= chip_rows), 1.0, 0.0)).astype(jnp.int32)
    a = jnp.where(crosses, a, 0)
    b = jnp.where(crosses, b, 0)
    ka = lax.div(a + UNIT - 1, UNIT)
    kb = lax.div(b + UNIT - 1, UNIT)
    least = jnp.int32(0)
    most = jnp.int32(0)
    for h in range(heads):
        least += (ka * (heads - h) > budget).astype(jnp.int32)
        most += (kb * (h + 1) <= budget).astype(jnp.int32)
    plan_ref[0] = lax.div(lax.axis_index("seq"), CORES)
    plan_ref[1] = core
    plan_ref[2] = a
    plan_ref[3] = b
    plan_ref[4] = ka
    plan_ref[5] = kb
    plan_ref[6] = jnp.minimum(jnp.maximum(heads // 2, least), most)
    plan_ref[7] = crosses.astype(jnp.int32)
    plan_ref[8] = jnp.int32(heads)
    plan_ref[9] = jnp.int32(chip_rows)

    for copy in gain_copies:
        copy.wait()
    for n, (raw_ref, gain_ref) in enumerate(((q_ref, qg_ref), (k_ref, kg_ref))):
        for step in range(steps):
            raw_copies[n * steps + step].wait()
            here = pl.ds(step * part, part)
            raw = raw_ref[here, :].astype(jnp.float32)
            inv = lax.rsqrt(jnp.mean(raw * raw, axis=-1, keepdims=True) + EPSILON)
            inv_ref[n, here, :] = jnp.broadcast_to(inv, (part, D_HEAD))
            normed = (raw * inv * gain_ref[...]).astype(jnp.bfloat16)
            pieces = [normed[:, j * D_HEAD : (j + 1) * D_HEAD] for j in range(2 * heads)]

            @pl.when(core == 0)
            def _():
                for j in range(heads):
                    mine_ref[n, j, here, :] = pieces[j]
                    theirs_ref[n, j, here, :] = pieces[heads + j]

            @pl.when(core == 1)
            def _():
                for j in range(heads):
                    mine_ref[n, j, here, :] = pieces[heads + j]
                    theirs_ref[n, j, here, :] = pieces[j]

    for copy in head_copies:
        copy.wait()


def pack_kernel(rows, plan, mine_ref, got_ref, *send_refs):
    core = plan[1]
    j0, j1, k_own, row0 = own_side(plan)
    first_units = send_refs[0].shape[1] // UNIT
    for ref, half in ((mine_ref, core), (got_ref, 1 - core)):
        base = half * rows
        low = jnp.clip(lax.div(base - row0, UNIT), 0, k_own)
        high = jnp.clip(lax.div(base + rows - row0, UNIT), 0, k_own)

        def one_head(j, _, ref=ref, base=base, low=low, high=high):
            start = (j - j0) * k_own
            cut = jnp.clip(first_units - start, low, high)

            def unit_into(send_ref, shift):
                def one_unit(i, _):
                    at = pl.multiple_of(row0 + UNIT * i - base, UNIT)
                    to = pl.multiple_of((start + i - shift) * UNIT, UNIT)
                    for n in range(4):
                        send_ref[n, pl.ds(to, UNIT), :] = ref[n, j, pl.ds(at, UNIT), :]
                    return 0

                return one_unit

            lax.fori_loop(low, cut, unit_into(send_refs[0], 0), 0)
            if len(send_refs) > 1:
                lax.fori_loop(cut, high, unit_into(send_refs[1], first_units), 0)
            return 0

        lax.fori_loop(j0, j1, one_head, 0)


def local_kernel(rows, heads, group, plan, mine_ref, got_ref, seg_ref, vis_ref, qg_ref, kg_ref,
                 keep_ref, give_ref, gain_ref, cross_bias_ref, bias_ref, ok_ref):
    both = 2 * rows
    core, first = plan[1], plan[0] * both

    def chip_row(ref):
        wide = ref[...].astype(jnp.float32)
        total = wide.shape[1]
        wide = jnp.broadcast_to(wide, (8, total))
        own = pltpu.roll(wide, lax.rem(2 * total - first - core * rows, total), 1)
        other = pltpu.roll(wide, lax.rem(2 * total - first - (1 - core) * rows, total), 1)
        return jnp.concatenate([own[:, :rows], other[:, :rows]], axis=1)[0:1]

    seg = jnp.broadcast_to(chip_row(seg_ref), (both, both))
    code = jnp.broadcast_to(chip_row(seg_ref) * 2.0 + chip_row(vis_ref), (both, both))
    code_t = jnp.transpose(code)
    i = lax.broadcasted_iota(jnp.int32, (both, both), 0)
    j = lax.broadcasted_iota(jnp.int32, (both, both), 1)
    gap = code_t - 2.0 * seg
    allowed = (gap == 1.0) | (i == j)
    bias_ref[...] = jnp.where(allowed, 0.0, NEG)
    r = lax.broadcasted_iota(jnp.int32, (both, D_HEAD), 0)
    at = jnp.where(r < rows, core * rows + r, (1 - core) * rows + r - rows) + first
    edge = plan[9]
    crossing = (at >= edge - plan[2]) & (at < edge + plan[3])
    ok_ref[...] = jnp.where(crossing, 0.0, 1.0)
    wide = vis_ref[...].astype(jnp.float32)
    total = wide.shape[1]
    vis = pltpu.roll(jnp.broadcast_to(wide, (8, total)), lax.rem(total - edge + plan[2], total), 1)
    vis = jnp.transpose(jnp.broadcast_to(vis[0:1, :both], (both, both))) > 0.5
    length = plan[2] + plan[3]
    allowed = (i == j) | ((i < length) & (j < length) & vis)
    cross_bias_ref[...] = jnp.where(allowed, 0.0, NEG)

    def some_heads(step, _):
        for h in range(group):
            j = step * group + h
            q, k, v, g = (
                jnp.concatenate([mine_ref[n, j], got_ref[n, j]], axis=0) for n in range(4)
            )
            results = attention(q, k, v, g, bias_ref[...])
            for n, x in enumerate(results):
                keep_ref[n, j] = x[:rows]
                give_ref[n, j] = x[rows:]
            col = pl.ds(pl.multiple_of((core * heads + j) * D_HEAD, D_HEAD), D_HEAD)
            ok = ok_ref[...]
            for n, (x, y, gain) in enumerate(
                ((q, results[1], qg_ref), (k, results[2], kg_ref))
            ):
                term = ok * x.astype(jnp.float32) * y.astype(jnp.float32)
                gain_ref[n, pl.ds(j, 1), :] = jnp.sum(term, axis=0, keepdims=True) / gain[:, col]
        return 0

    lax.fori_loop(0, heads // group, some_heads, 0)


def crossing_kernel(rows, heads, stage, stages, group, plan, mine_ref, got_ref, far_refs, bias_ref,
                    qg_ref, kg_ref, gain_in, keep_ref, give_ref, gain_ref, back_ref, seq_ref,
                    res_ref):
    both = 2 * rows
    chip, core = plan[0], plan[1]
    a, b = plan[2], plan[3]
    first = chip == 0
    edge = plan[9]
    start = edge - a
    own_lo = chip * both
    k_far = jnp.where(first, plan[5], plan[4])
    far_row0 = jnp.where(first, edge, edge - UNIT * plan[4])
    j0 = jnp.where(first, 0, plan[6])
    count = jnp.where(plan[7] == 1, jnp.where(first, plan[6], heads - plan[6]), 0)
    first_units = far_refs[0].shape[1] // UNIT
    if stages == 1:
        low, high = 0, count
    else:
        ready = jnp.minimum(lax.div(first_units, jnp.maximum(k_far, 1)), count)
        low, high = (0, ready) if stage == 0 else (ready, count)

    gain_ref[...] = gain_in[...]
    own_at = pl.multiple_of(own_lo + core * rows, rows)
    got_at = pl.multiple_of(own_lo + (1 - core) * rows, rows)

    def some_heads(step, _):
        places = [jnp.minimum(low + step * group + s, high - 1) for s in range(group)]
        for s, jj in enumerate(places):
            j = j0 + jj
            for n in range(4):
                seq_ref[s, n, pl.ds(own_at, rows), :] = mine_ref[n, j].astype(jnp.float32)
                seq_ref[s, n, pl.ds(got_at, rows), :] = got_ref[n, j].astype(jnp.float32)

            def load_from(far_ref, shift, s=s, jj=jj):
                def load(i, _):
                    at = pl.multiple_of((jj * k_far + i - shift) * UNIT, UNIT)
                    to = pl.multiple_of(far_row0 + UNIT * i, UNIT)
                    for n in range(4):
                        seq_ref[s, n, pl.ds(to, UNIT), :] = far_ref[n, pl.ds(at, UNIT), :].astype(
                            jnp.float32
                        )
                    return 0

                return load

            if stage == 0:
                lax.fori_loop(0, k_far, load_from(far_refs[0], 0), 0)
            else:
                cut = jnp.clip(first_units - jj * k_far, 0, k_far)
                lax.fori_loop(0, cut, load_from(far_refs[0], 0), 0)
                lax.fori_loop(cut, k_far, load_from(far_refs[1], first_units), 0)
        for s, jj in enumerate(places):
            j = j0 + jj
            inside = lax.broadcasted_iota(jnp.int32, (both, D_HEAD), 0) < a + b
            q, k, v, g = (
                jnp.where(inside, seq_ref[s, n, pl.ds(start, both), :], 0.0).astype(jnp.bfloat16)
                for n in range(4)
            )
            results = attention(q, k, v, g, bias_ref[...])
            for n, x in enumerate(results):
                res_ref[s, n, pl.ds(start, both), :] = x.astype(jnp.float32)
            col = pl.ds(pl.multiple_of((core * heads + j) * D_HEAD, D_HEAD), D_HEAD)
            for n, (x, y, gain) in enumerate(
                ((q, results[1], qg_ref), (k, results[2], kg_ref))
            ):
                term = x.astype(jnp.float32) * y.astype(jnp.float32)
                gain_ref[n, pl.ds(j, 1), :] = (
                    gain_in[n, pl.ds(j, 1), :] + jnp.sum(term, axis=0, keepdims=True) / gain[:, col]
                )
        for s, jj in enumerate(places):
            j = j0 + jj
            r = lax.broadcasted_iota(jnp.int32, (rows, D_HEAD), 0)
            for at, ref in ((own_at, keep_ref), (got_at, give_ref)):
                inside = (r + at >= start) & (r + at < edge + b)
                for n in range(4):
                    x = res_ref[s, n, pl.ds(at, rows), :]
                    old = ref[n, j].astype(jnp.float32)
                    ref[n, j] = jnp.where(inside, x, old).astype(jnp.bfloat16)

            def store(i, _, s=s, jj=jj):
                to = pl.multiple_of((jj * k_far + i) * UNIT, UNIT)
                at = pl.multiple_of(far_row0 + UNIT * i, UNIT)
                for n in range(4):
                    back_ref[n, pl.ds(to, UNIT), :] = res_ref[s, n, pl.ds(at, UNIT), :].astype(
                        jnp.bfloat16
                    )
                return 0

            lax.fori_loop(0, k_far, store, 0)
        return 0

    lax.fori_loop(0, lax.div(high - low + group - 1, group), some_heads, 0)


def assemble_kernel(heads, plan, keep_ref, got_ref, *to_refs):
    core = plan[1]
    for ref, side in ((keep_ref, core), (got_ref, 1 - core)):
        for j in range(heads):
            col = pl.multiple_of((side * heads + j) * D_HEAD, D_HEAD)
            for n in range(4):
                to_refs[n][:, pl.ds(col, D_HEAD)] = ref[n, j]


def join_kernel(heads, plan, own_ref, got_ref, to_ref):
    to_ref[:, pl.ds(pl.multiple_of(plan[1] * heads, heads), heads), :] = own_ref[...]
    to_ref[:, pl.ds(pl.multiple_of((1 - plan[1]) * heads, heads), heads), :] = got_ref[...]


def add_kernel(x_ref, y_ref, to_ref):
    to_ref[...] = x_ref[...] + y_ref[...]


def finish_kernel(rows, heads, plan, q_ref, k_ref, qg_ref, kg_ref, inv_ref, back_ref,
                  back_got_ref, *rest):
    out_hbm, dq_hbm, dk_hbm, dv_hbm, *held = rest[4:12]
    wide_ref, dq_ref, dk_ref, sems = rest[12:]
    core = plan[1]
    j0, j1, k_own, row0 = own_side(plan)
    base = core * rows
    length = back_ref.shape[1]
    for s, ref in enumerate((back_ref, back_got_ref)):
        wide_ref[s, :, pl.ds(rows, length), :] = ref[...]
    r = lax.broadcasted_iota(jnp.int32, (rows, D_HEAD), 0) + base
    first = plan[0] == 0
    inside = (r >= jnp.where(first, plan[9] - plan[2], 0)) & (
        r < jnp.where(first, plan[9], plan[3])
    )

    def one_head(j, _):
        at = (j - j0) * k_own * UNIT + base - row0 + rows
        at = pl.multiple_of(jnp.clip(at, 0, length + rows), UNIT)
        for s, side in ((0, core), (1, 1 - core)):
            col = pl.multiple_of((side * heads + j) * D_HEAD, D_HEAD)
            for n in range(4):
                new = wide_ref[s, n, pl.ds(at, rows), :].astype(jnp.float32)
                old = held[n][:, pl.ds(col, D_HEAD)].astype(jnp.float32)
                held[n][:, pl.ds(col, D_HEAD)] = jnp.where(inside, new, old).astype(jnp.bfloat16)
        return 0

    lax.fori_loop(j0, jnp.where(k_own > 0, j1, j0), one_head, 0)
    copies = [
        pltpu.make_async_copy(held[0], out_hbm, sems.at[0]),
        pltpu.make_async_copy(held[3], dv_hbm, sems.at[1]),
        pltpu.make_async_copy(dq_ref, dq_hbm, sems.at[2]),
        pltpu.make_async_copy(dk_ref, dk_hbm, sems.at[3]),
    ]
    copies[0].start()
    copies[1].start()
    for n, (raw_ref, gain_ref, grad_ref, to_ref) in enumerate(
        ((q_ref, qg_ref, held[1], dq_ref), (k_ref, kg_ref, held[2], dk_ref))
    ):
        raw = raw_ref[...].astype(jnp.float32)
        scaled = gain_ref[...] * grad_ref[...].astype(jnp.float32)
        mean_term = jnp.mean(scaled * raw, axis=-1, keepdims=True)
        inv = inv_ref[n, :, 0:1]
        to_ref[...] = (inv * scaled - raw * (inv * inv * inv * mean_term)).astype(jnp.bfloat16)
        copies[2 + n].start()
    for copy in copies:
        copy.wait()


def per_device_clips(queries, keys, values, q_gain, k_gain, out_grad, segments, visible, dp):
    rows, width = queries.shape
    heads = width // D_HEAD // CORES
    seq = segments.shape[1]
    budget = units_needed(CORES * rows // UNIT, heads)
    both = CORES * rows
    bf16, f32 = jnp.bfloat16, jnp.float32
    smem = pl.BlockSpec(memory_space=pltpu.SMEM)
    vmem = pl.BlockSpec(memory_space=pltpu.VMEM)
    hbm = pl.BlockSpec(memory_space=pl.ANY)
    limit = lambda mib: pltpu.CompilerParams(vmem_limit_bytes=mib << 20)
    keep_in_vmem = lambda x: pltpu.with_memory_space_constraint(x, pltpu.VMEM)
    swap_core = [(i, i ^ 1) for i in range(4)]
    swap_chip = [(i, i ^ 2) for i in range(4)]
    q_gain2, k_gain2 = q_gain[None], k_gain[None]
    split = pltpu.VMEM((4, heads, rows, D_HEAD), bf16)

    hbm_only = pl.BlockSpec(memory_space=pltpu.HBM)
    mine, theirs, inv, plan = pl.pallas_call(
        functools.partial(prepare_kernel, rows, heads, budget, PREPARE_STEPS),
        in_specs=[hbm_only] * 7,
        out_specs=[vmem, vmem, vmem, smem],
        out_shape=[
            split,
            split,
            pltpu.VMEM((2, rows, D_HEAD), f32),
            jax.ShapeDtypeStruct((16,), jnp.int32),
        ],
        scratch_shapes=[
            pltpu.VMEM((rows, width), bf16),
            pltpu.VMEM((rows, width), bf16),
            pltpu.VMEM((1, width), f32),
            pltpu.VMEM((1, width), f32),
            pltpu.VMEM((1, seq), jnp.int32),
            pltpu.SemaphoreType.DMA((3 + 2 * PREPARE_STEPS,)),
            pltpu.SemaphoreType.DMA((4 * heads,)),
        ],
        compiler_params=limit(16),
        name="prepare",
    )(*[pltpu.with_memory_space_constraint(x, pltpu.HBM)
        for x in (queries, keys, values, out_grad, q_gain2, k_gain2, segments)])
    got = keep_in_vmem(lax.ppermute(theirs, "seq", swap_core))
    mine = keep_in_vmem(mine)

    sizes = [budget] if FIRST_UNITS is None else [FIRST_UNITS, budget - FIRST_UNITS]
    sends = pl.pallas_call(
        functools.partial(pack_kernel, rows),
        in_specs=[smem, vmem, vmem],
        out_specs=[vmem] * len(sizes),
        out_shape=[pltpu.VMEM((4, n * UNIT, D_HEAD), bf16) for n in sizes],
        compiler_params=limit(4),
        name="pack",
    )(plan, mine, got)
    fars = [keep_in_vmem(lax.ppermute(x, "seq", swap_chip)) for x in sends]

    gains_shape = pltpu.VMEM((2, heads, D_HEAD), f32)
    keep, give, gain_part, cross_bias = pl.pallas_call(
        functools.partial(local_kernel, rows, heads, LOCAL_GROUP),
        in_specs=[smem] + [vmem] * 6,
        out_specs=[vmem] * 4,
        out_shape=[split, split, gains_shape, pltpu.VMEM((both, both), f32)],
        scratch_shapes=[pltpu.VMEM((both, both), f32), pltpu.VMEM((both, D_HEAD), f32)],
        compiler_params=limit(16),
        name="local",
    )(plan, mine, got, segments, visible, q_gain2, k_gain2)

    back_shape = pltpu.VMEM((4, budget * UNIT, D_HEAD), bf16)
    back = None
    for stage in range(len(sizes)):
        args = [plan, mine, got, *fars[: stage + 1], keep_in_vmem(cross_bias), q_gain2, k_gain2]
        args += [keep_in_vmem(x) for x in (gain_part, keep, give)]
        aliases = {len(args) - 2: 0, len(args) - 1: 1}
        if stage:
            aliases[len(args)] = 3
            args.append(keep_in_vmem(back))

        def body(*refs, stage=stage, count=len(args)):
            ins, outs = refs[:count], refs[count:]
            far = ins[3 : 4 + stage]
            vis, qg, kg, gain_in = ins[4 + stage : 8 + stage]
            crossing_kernel(rows, heads, stage, len(sizes), CROSS_GROUPS[stage], ins[0], ins[1], ins[2],
                            far, vis, qg, kg, gain_in, *outs)

        keep, give, gain_part, back = pl.pallas_call(
            body,
            in_specs=[smem] + [vmem] * (len(args) - 1),
            out_specs=[vmem] * 4,
            out_shape=[split, split, gains_shape, back_shape],
            input_output_aliases=aliases,
            scratch_shapes=[
                pltpu.VMEM((CROSS_GROUPS[stage], 4, seq, D_HEAD), f32),
                pltpu.VMEM((CROSS_GROUPS[stage], 4, seq, D_HEAD), f32),
            ],
            compiler_params=limit(20),
        )(*args)

    back = lax.ppermute(back, "seq", swap_chip)
    res_got = keep_in_vmem(lax.ppermute(give, "seq", swap_core))
    gain_got = lax.ppermute(gain_part, "seq", swap_core)
    total_shape = pltpu.VMEM((2, CORES * heads, D_HEAD), f32)
    total = pl.pallas_call(
        functools.partial(join_kernel, heads),
        in_specs=[smem, vmem, vmem],
        out_specs=vmem,
        out_shape=total_shape,
        compiler_params=limit(1),
        name="join",
    )(plan, keep_in_vmem(gain_part), keep_in_vmem(gain_got))
    step = 1
    while step < dp:
        total_got = lax.ppermute(total, "dp", [(i, i ^ step) for i in range(dp)])
        total = pl.pallas_call(
            add_kernel,
            in_specs=[vmem, vmem],
            out_specs=vmem,
            out_shape=total_shape,
            compiler_params=limit(1),
            name="add",
        )(keep_in_vmem(total), keep_in_vmem(total_got))
        step *= 2

    held = pl.pallas_call(
        functools.partial(assemble_kernel, heads),
        in_specs=[smem, vmem, vmem],
        out_specs=[vmem] * 4,
        out_shape=[pltpu.VMEM((rows, width), bf16)] * 4,
        compiler_params=limit(4),
        name="assemble",
    )(plan, keep_in_vmem(keep), res_got)

    back, total, held = lax.optimization_barrier((back, total, held))
    back_got = keep_in_vmem(lax.ppermute(back, "seq", swap_core))
    total_got = lax.ppermute(total, "seq", swap_chip)

    full = jax.ShapeDtypeStruct((rows, width), bf16)
    outs = pl.pallas_call(
        functools.partial(finish_kernel, rows, heads),
        in_specs=[smem] + [vmem] * 11,
        out_specs=[hbm] * 4 + [vmem] * 4,
        out_shape=[full] * 4 + [pltpu.VMEM((rows, width), bf16)] * 4,
        input_output_aliases={8 + i: 4 + i for i in range(4)},
        scratch_shapes=[
            pltpu.VMEM((2, 4, budget * UNIT + 2 * rows, D_HEAD), bf16),
            pltpu.VMEM((rows, width), bf16),
            pltpu.VMEM((rows, width), bf16),
            pltpu.SemaphoreType.DMA((4,)),
        ],
        compiler_params=limit(12),
        name="finish",
    )(plan, keep_in_vmem(queries), keep_in_vmem(keys), q_gain2, k_gain2, keep_in_vmem(inv), keep_in_vmem(back), back_got,
      *[keep_in_vmem(x) for x in held])
    attn_out, query_grad, key_grad, value_grad = outs[:4]
    total = total + total_got
    return (attn_out, query_grad, key_grad, value_grad, total[0].reshape(width), total[1].reshape(width))


def solution(mesh):
    dp, seq = mesh.shape["dp"], mesh.shape["seq"]
    two_chips = seq == 2 * CORES and dp & (dp - 1) == 0

    def per_device(queries, keys, values, q_gain, k_gain, out_grad, segments, visible):
        args = (queries, keys, values, q_gain, k_gain, out_grad, segments, visible)
        if two_chips:
            return per_device_clips(*args, dp)
        return per_device_any(*args)

    rows = P(("dp", "seq"), None)
    return jax.shard_map(
        per_device,
        mesh=mesh,
        in_specs=(rows, rows, rows, P(), P(), rows, P("dp", None), P("dp", None)),
        out_specs=(rows, rows, rows, rows, P(), P()),
        check_vma=False,
    )
```

time: 165 us -> 51.5 us (0.31)
  blocking collectives: 40.3 us -> 0 us
  matrix products: 29.5 us -> 0 us
  waiting for transfers between devices: 39.1 us -> 21.3 us
  starting transfers between devices: 29.4 us -> 14.4 us
  local copies, waits for them, and re-layouts: 15.6 us -> 0.64 us
  Pallas kernels: 0 us -> 14.3 us
  other arithmetic: 9.54 us -> 0.01 us
    psum x1 -> x0, blocking collectives: 40.3 us -> none  [per_device(): lax.psum((q_gain_part, k_gain_part), ('dp', 'seq'))]
    all_to_all x8 -> x0, waiting for transfers between devices: 39.1 us -> none  [the longest x1 7.93 us: per_device(): lax.all_to_all(k_norm, 'seq', split_axis=1, concat_axis=0, tiled=True)]
    all_to_all x8 -> x0, starting transfers between devices: 29.4 us -> none  [the longest x1 4.32 us: per_device(): lax.all_to_all(q_part, 'seq', split_axis=0, concat_axis=1, tiled=True)]
    dot_general x5 -> x0, matrix products: 24.8 us -> none  [the longest x1 8.53 us: one_block(): jnp.einsum('hst,thd->shd', score_grad, k_three, preferred_element_type=jn...]
    ppermute x0 -> x11, waiting for transfers between devices: none -> 21.3 us  [the longest x3 8.07 us: per_device_clips(): total_got = lax.ppermute(total, 'dp', [(i, i ^ step) for i in range(dp)])]
    ppermute x0 -> x11, starting transfers between devices: none -> 14.4 us  [the longest x3 7.19 us: per_device_clips(): total_got = lax.ppermute(total, 'dp', [(i, i ^ step) for i in range(dp)])]
    pallas_call x0 -> x11, Pallas kernels: none -> 14.3 us  [the longest x1 5.36 us: per_device_clips(): pl.pallas_call(functools.partial(local_kernel, rows, heads, LOCAL_GROUP),...]
    convert_element_type x10 -> x0, local copies, waits for them, and re-layouts: 7.69 us -> none  [the longest x2 2.03 us: one_block(): q_grad = jnp.einsum('hst,thd->shd', score_grad, k_three, preferred_elemen...]
  transfers between devices with their start and end apart: 8 -> 11, of which waited for: 6 -> 8; matrix products, arithmetic and copies ran while one was open for 22% -> 1% of each run, Pallas kernels for 0% -> 15%
where the time goes in v1:
time: 51.5 us; the launch traced here: 51.3 us
  waiting for transfers between devices  21.3 us (41%)
  starting transfers between devices  14.4 us (28%)
  Pallas kernels  14.3 us (28%)
  between operations  0.76 us (1%)
  local copies, waits for them, and re-layouts  0.64 us (1%)
    ppermute x3, waiting for transfers between devices, per_device_clips(): total_got = lax.ppermute(total, 'dp', [(i, i ^ step) for i in range(dp)])  8.07 us
    ppermute x2, waiting for transfers between devices, per_device_clips(): fars = [keep_in_vmem(lax.ppermute(x, 'seq', swap_chip)) for x in sends]  7.6 us
    ppermute x3, starting transfers between devices, per_device_clips(): total_got = lax.ppermute(total, 'dp', [(i, i ^ step) for i in range(dp)])  7.19 us
    pallas_call x1, Pallas kernels, per_device_clips(): pl.pallas_call(functools.partial(local_kernel, rows, heads, LOCAL_GROUP),...  5.36 us
    pallas_call x1, Pallas kernels, per_device_clips(): pl.pallas_call(functools.partial(prepare_kernel, rows, heads, budget, PRE...  3.14 us
    ppermute x2, starting transfers between devices, per_device_clips(): fars = [keep_in_vmem(lax.ppermute(x, 'seq', swap_chip)) for x in sends]  3.02 us
    ppermute x1, waiting for transfers between devices, per_device_clips(): total_got = lax.ppermute(total, 'seq', swap_chip)  2.32 us
    ppermute x1, waiting for transfers between devices, per_device_clips(): got = keep_in_vmem(lax.ppermute(theirs, 'seq', swap_core))  2.29 us
  transfers between devices with their start and end apart: 11, of which 8 were waited for; matrix products, arithmetic and copies ran while one was open for 1% of the time, Pallas kernels for 15%

profile of v1, /device:TPU:0, one launch (start us, length us, event | category | flops | bytes accessed | tf_op | source)
XLA Modules:
  0.0 51.3 jit_solution(3493060084012075589)
XLA Ops:
  0.6 3.1 %prepare.1 = (bf16[4,8,128,128]{3,2,1,0:T(8,128)(2,1)S(1)}, bf16[4,8,128,128]{3,2,1,0:T(8,128)(2,1)S(1)}, f32[2,128,128]{2,1,0:T(8,128)S(1)}, s32[16]{0:T(128)S(1)}) custom-call(bf16[128,2048]{1,0:T(8,128)(2,1)} %q_ref.1, bf16[128,2048]{1,0:T(8,128)(2,1)} %k_ref.1, bf16[128,2048]{1,0:T(8,128)(2,1)} %v_hbm.1, bf16[128,2048]{1,0:T(8,128)(2,1)} %g_hbm.1, ...), custom_call_target="tpu_custom_call" | custom-call | tf_op jit(solution)/shard_map/prepare/pallas_call | solution.py:483
  3.8 0.6 %collective-permute-start = (bf16[4,8,128,128]{3,2,1,0:T(8,128)(2,1)S(1)}, bf16[4,8,128,128]{3,2,1,0:T(8,128)(2,1)S(1)}, u32[]{:S(2)}, u32[]{:S(2)}) collective-permute-start(bf16[4,8,128,128]{3,2,1,0:T(8,128)(2,1)S(1)} %get-tuple-element.41), channel_id=1, source_target_pairs={{0,1},{1,0},{2,3},{3,2},{4,5},{5,4},{6,7},{7,6},{8,9},{9,8},{10,11... | collective-permute-start | bytes 3145736 | tf_op jit(solution)/shard_map/ppermute | solution.py:506
  4.3 2.3 %collective-permute-done.got_ref.refs_2_ = bf16[4,8,128,128]{3,2,1,0:T(8,128)(2,1)S(1)} collective-permute-done((bf16[4,8,128,128]{3,2,1,0:T(8,128)(2,1)S(1)}, bf16[4,8,128,128]{3,2,1,0:T(8,128)(2,1)S(1)}, u32[]{:S(2)}, u32[]{:S(2)}) %collective-permute-start) | collective-permute-done | bytes 1048608 | tf_op jit(solution)/shard_map/ppermute | solution.py:506
  6.6 0.7 %pack.1 = (bf16[4,432,128]{2,1,0:T(8,128)(2,1)S(1)}, bf16[4,144,128]{2,1,0:T(8,128)(2,1)S(1)}) custom-call(s32[16]{0:T(128)S(1)} %get-tuple-element.38.plan.refs_0_, bf16[4,8,128,128]{3,2,1,0:T(8,128)(2,1)S(1)} %get-tuple-element.40.mine_ref.refs_1_, bf16[4,8,128,128]{3,2,1,0:T(8,128)(2,1)S(1)} %collective-permute-done.got_ref.refs_2_), custom_call_target="tpu_custom_call" | custom-call | tf_op jit(solution)/shard_map/pack/pallas_call | solution.py:510
  7.4 2.9 %collective-permute-start.1 = (bf16[4,432,128]{2,1,0:T(8,128)(2,1)S(1)}, bf16[4,432,128]{2,1,0:T(8,128)(2,1)S(1)}, u32[]{:S(2)}, u32[]{:S(2)}) collective-permute-start(bf16[4,432,128]{2,1,0:T(8,128)(2,1)S(1)} %get-tuple-element.42), channel_id=1, source_target_pairs={{0,2},{1,3},{2,0},{3,1},{4,6},{5,7},{6,4},{7,5},{8,10},{9,11},{10,... | collective-permute-start | bytes 1327112 | tf_op jit(solution)/shard_map/ppermute | solution.py:518
  10.4 5.4 %local.1 = (bf16[4,8,128,128]{3,2,1,0:T(8,128)(2,1)S(1)}, bf16[4,8,128,128]{3,2,1,0:T(8,128)(2,1)S(1)}, f32[2,8,128]{2,1,0:T(8,128)S(1)}, f32[256,256]{1,0:T(8,128)S(1)}) custom-call(s32[16]{0:T(128)S(1)} %get-tuple-element.38.plan.refs_0_, bf16[4,8,128,128]{3,2,1,0:T(8,128)(2,1)S(1)} %get-tuple-element.40.mine_ref.refs_1_, ...), custom_call_target="tpu_custom_call" | custom-call | tf_op jit(solution)/shard_map/local/pallas_call | solution.py:521
  15.8 5.6 %collective-permute-done.1.refs_3_ = bf16[4,432,128]{2,1,0:T(8,128)(2,1)S(1)} collective-permute-done((bf16[4,432,128]{2,1,0:T(8,128)(2,1)S(1)}, bf16[4,432,128]{2,1,0:T(8,128)(2,1)S(1)}, u32[]{:S(2)}, u32[]{:S(2)}) %collective-permute-start.1) | collective-permute-done | bytes 442400 | tf_op jit(solution)/shard_map/ppermute | solution.py:518
  21.3 0.6 %shard_map.127 = (bf16[4,8,128,128]{3,2,1,0:T(8,128)(2,1)S(1)}, bf16[4,8,128,128]{3,2,1,0:T(8,128)(2,1)S(1)}, f32[2,8,128]{2,1,0:T(8,128)S(1)}, bf16[4,576,128]{2,1,0:T(8,128)(2,1)S(1)}) custom-call(s32[16]{0:T(128)S(1)} %get-tuple-element.38.plan.refs_0_, ...), custom_call_target="tpu_custom_call", output_to_operand_aliasing={{0}: (8, {}), {1}: (9, {})} | custom-call | tf_op jit(solution)/shard_map/pallas_call | solution.py:548
  21.9 2.0 %collective-permute-done.2.refs_4_ = bf16[4,144,128]{2,1,0:T(8,128)(2,1)S(1)} collective-permute-done((bf16[4,144,128]{2,1,0:T(8,128)(2,1)S(1)}, bf16[4,144,128]{2,1,0:T(8,128)(2,1)S(1)}, u32[]{:S(2)}, u32[]{:S(2)}) %collective-permute-start.2) | collective-permute-done | bytes 147488 | tf_op jit(solution)/shard_map/ppermute | solution.py:518
  24.0 0.6 %shard_map.128 = (bf16[4,8,128,128]{3,2,1,0:T(8,128)(2,1)S(1)}, bf16[4,8,128,128]{3,2,1,0:T(8,128)(2,1)S(1)}, f32[2,8,128]{2,1,0:T(8,128)S(1)}, bf16[4,576,128]{2,1,0:T(8,128)(2,1)S(1)}) custom-call(s32[16]{0:T(128)S(1)} %get-tuple-element.38.plan.refs_0_, ...), custom_call_target="tpu_custom_call", output_to_operand_aliasing={{0}: (9, {}), {1}: (10, {}), {3}: (11, {})} | custom-call | tf_op jit(solution)/shard_map/pallas_call | solution.py:548
  24.6 1.8 %collective-permute-start.3 = (bf16[4,576,128]{2,1,0:T(8,128)(2,1)S(1)}, bf16[4,576,128]{2,1,0:T(8,128)(2,1)S(1)}, u32[]{:S(2)}, u32[]{:S(2)}) collective-permute-start(bf16[4,576,128]{2,1,0:T(8,128)(2,1)S(1)} %get-tuple-element.52), channel_id=1, source_target_pairs={{0,2},{1,3},{2,0},{3,1},{4,6},{5,7},{6,4},{7,5},{8,10},{9,11},{10,... | collective-permute-start | bytes 1769480 | tf_op jit(solution)/shard_map/ppermute | solution.py:561
  26.4 0.2 collective-permute-start.4
  26.6 1.0 %collective-permute-done.4.got_ref = f32[2,8,128]{2,1,0:T(8,128)S(1)} collective-permute-done((f32[2,8,128]{2,1,0:T(8,128)S(1)}, f32[2,8,128]{2,1,0:T(8,128)S(1)}, u32[]{:S(2)}, u32[]{:S(2)}) %collective-permute-start.4) | collective-permute-done | bytes 8224 | tf_op jit(solution)/shard_map/ppermute | solution.py:563
  27.6 0.5 %join.1.x_ref = f32[2,16,128]{2,1,0:T(8,128)S(1)} custom-call(s32[16]{0:T(128)S(1)} %get-tuple-element.38.plan.refs_0_, f32[2,8,128]{2,1,0:T(8,128)S(1)} %get-tuple-element.53.own_ref, f32[2,8,128]{2,1,0:T(8,128)S(1)} %collective-permute-done.4.got_ref), custom_call_target="tpu_custom_call" | custom-call | tf_op jit(solution)/shard_map/join/pallas_call | solution.py:565
  28.1 5.0 %collective-permute-start.5 = (f32[2,16,128]{2,1,0:T(8,128)S(1)}, f32[2,16,128]{2,1,0:T(8,128)S(1)}, u32[]{:S(2)}, u32[]{:S(2)}) collective-permute-start(f32[2,16,128]{2,1,0:T(8,128)S(1)} %join.1.x_ref), channel_id=1, source_target_pairs={{0,4},{4,0},{8,12},{12,8},{16,20},{20,16},{24,28},{28,24},{1,5},{5... | collective-permute-start | bytes 49160 | tf_op jit(solution)/shard_map/ppermute | solution.py:575
  33.1 1.7 %collective-permute-done.5.y_ref = f32[2,16,128]{2,1,0:T(8,128)S(1)} collective-permute-done((f32[2,16,128]{2,1,0:T(8,128)S(1)}, f32[2,16,128]{2,1,0:T(8,128)S(1)}, u32[]{:S(2)}, u32[]{:S(2)}) %collective-permute-start.5) | collective-permute-done | bytes 16416 | tf_op jit(solution)/shard_map/ppermute | solution.py:575
  34.8 2.2 %collective-permute-start.6 = (f32[2,16,128]{2,1,0:T(8,128)S(1)}, f32[2,16,128]{2,1,0:T(8,128)S(1)}, u32[]{:S(2)}, u32[]{:S(2)}) collective-permute-start(f32[2,16,128]{2,1,0:T(8,128)S(1)} %add.7.x_ref), channel_id=1, source_target_pairs={{0,8},{4,12},{8,0},{12,4},{16,24},{20,28},{24,16},{28,20},{1,9},{5... | collective-permute-start | bytes 49160 | tf_op jit(solution)/shard_map/ppermute | solution.py:575
  37.0 1.7 %collective-permute-done.6.y_ref = f32[2,16,128]{2,1,0:T(8,128)S(1)} collective-permute-done((f32[2,16,128]{2,1,0:T(8,128)S(1)}, f32[2,16,128]{2,1,0:T(8,128)S(1)}, u32[]{:S(2)}, u32[]{:S(2)}) %collective-permute-start.6) | collective-permute-done | bytes 16416 | tf_op jit(solution)/shard_map/ppermute | solution.py:575
  38.8 4.6 %collective-permute-done.7.y_ref = f32[2,16,128]{2,1,0:T(8,128)S(1)} collective-permute-done((f32[2,16,128]{2,1,0:T(8,128)S(1)}, f32[2,16,128]{2,1,0:T(8,128)S(1)}, u32[]{:S(2)}, u32[]{:S(2)}) %collective-permute-start.7) | collective-permute-done | bytes 16416 | tf_op jit(solution)/shard_map/ppermute | solution.py:575
  43.4 1.1 %assemble.1 = (bf16[128,2048]{1,0:T(8,128)(2,1)S(1)}, bf16[128,2048]{1,0:T(8,128)(2,1)S(1)}, bf16[128,2048]{1,0:T(8,128)(2,1)S(1)}, bf16[128,2048]{1,0:T(8,128)(2,1)S(1)}) custom-call(s32[16]{0:T(128)S(1)} %get-tuple-element.38.plan.refs_0_, bf16[4,8,128,128]{3,2,1,0:T(8,128)(2,1)S(1)} %get-tuple-element.54.keep_ref, ...), custom_call_target="tpu_custom_call" | custom-call | tf_op jit(solution)/shard_map/assemble/pallas_call | solution.py:586
  44.7 1.5 %collective-permute-start.10 = (f32[2,16,128]{2,1,0:T(8,128)S(1)}, f32[2,16,128]{2,1,0:T(8,128)S(1)}, u32[]{:S(2)}, u32[]{:S(2)}) collective-permute-start(f32[2,16,128]{2,1,0:T(8,128)S(1)} %add.9), channel_id=1, source_target_pairs={{0,2},{1,3},{2,0},{3,1},{4,6},{5,7},{6,4},{7,5},{8,10},{9,11},{10,... | collective-permute-start | bytes 49160 | tf_op jit(solution)/shard_map/ppermute | solution.py:597
  46.2 2.3 %collective-permute-done.10 = f32[2,16,128]{2,1,0:T(8,128)S(1)} collective-permute-done((f32[2,16,128]{2,1,0:T(8,128)S(1)}, f32[2,16,128]{2,1,0:T(8,128)S(1)}, u32[]{:S(2)}, u32[]{:S(2)}) %collective-permute-start.10) | collective-permute-done | bytes 16416 | tf_op jit(solution)/shard_map/ppermute | solution.py:597
  48.5 0.6 %slice_bitcast_fusion = (f32[2048]{0:T(1024)}, f32[2048]{0:T(1024)}) fusion(f32[2,16,128]{2,1,0:T(8,128)S(1)} %add.6), kind=kLoop, calls=%fused_computation | loop fusion | bytes 32768 | tf_op jit(solution)/shard_map/reshape;squeeze | solution.py:618
  49.1 2.2 %finish.1 = (bf16[128,2048]{1,0:T(8,128)(2,1)}, bf16[128,2048]{1,0:T(8,128)(2,1)}, bf16[128,2048]{1,0:T(8,128)(2,1)}, bf16[128,2048]{1,0:T(8,128)(2,1)}, bf16[12...) custom-call(s32[16]{0:T(128)S(1)} %get-tuple-element.38.plan.refs_0_, ...), custom_call_target="tpu_custom_call", output_to_operand_aliasing={{4}: (8, {}), {5}: (9, {}), {6}: (10, {}), {7}: (11, {})} | custom-call | tf_op jit(solution)/shard_map/finish/pallas_call | solution.py:600
  (23 shorter events, 0.3 us)
Async XLA Ops:
  3.8 2.8 %collective-permute-start = (bf16[4,8,128,128]{3,2,1,0:T(8,128)(2,1)S(1)}, bf16[4,8,128,128]{3,2,1,0:T(8,128)(2,1)S(1)}, u32[]{:S(2)}, u32[]{:S(2)}) collective-permute-start(bf16[4,8,128,128]{3,2,1,0:T(8,128)(2,1)S(1)} %get-tuple-element.41), channel_id=1, source_target_pairs={{0,1},{1,0},{2,3},{3,2},{4,5},{5,4},{6,7},{7,6},{8,9},{9,8},{10,11... | collective-permute-start | bytes 3145736 | tf_op jit(solution)/shard_map/ppermute | solution.py:506
  6.6 3.8 %copy-start.2 = (f32[2048]{0:T(1024)S(1)}, f32[2048]{0:T(1024)}, u32[]{:S(2)}) copy-start(f32[2048]{0:T(1024)} %param.11) | copy-start | bytes 24580
  6.6 3.8 %copy-start.3 = (f32[2048]{0:T(1024)S(1)}, f32[2048]{0:T(1024)}, u32[]{:S(2)}) copy-start(f32[2048]{0:T(1024)} %param.12) | copy-start | bytes 24580
  6.6 3.8 %copy-start.5 = (s32[1,512]{1,0:T(1,128)S(1)}, s32[1,512]{1,0:T(1,128)}, u32[]{:S(2)}) copy-start(s32[1,512]{1,0:T(1,128)} %vis_ref.1) | copy-start | bytes 6148
  7.4 3.0 %copy-start.4 = (s32[1,512]{1,0:T(1,128)S(1)}, s32[1,512]{1,0:T(1,128)}, u32[]{:S(2)}) copy-start(s32[1,512]{1,0:T(1,128)} %seg_ref.1) | copy-start | bytes 6148
  7.4 14.0 %collective-permute-start.1 = (bf16[4,432,128]{2,1,0:T(8,128)(2,1)S(1)}, bf16[4,432,128]{2,1,0:T(8,128)(2,1)S(1)}, u32[]{:S(2)}, u32[]{:S(2)}) collective-permute-start(bf16[4,432,128]{2,1,0:T(8,128)(2,1)S(1)} %get-tuple-element.42), channel_id=1, source_target_pairs={{0,2},{1,3},{2,0},{3,1},{4,6},{5,7},{6,4},{7,5},{8,10},{9,11},{10,... | collective-permute-start | bytes 1327112 | tf_op jit(solution)/shard_map/ppermute | solution.py:518
  10.3 13.6 %collective-permute-start.2 = (bf16[4,144,128]{2,1,0:T(8,128)(2,1)S(1)}, bf16[4,144,128]{2,1,0:T(8,128)(2,1)S(1)}, u32[]{:S(2)}, u32[]{:S(2)}) collective-permute-start(bf16[4,144,128]{2,1,0:T(8,128)(2,1)S(1)} %get-tuple-element.43), channel_id=1, source_target_pairs={{0,2},{1,3},{2,0},{3,1},{4,6},{5,7},{6,4},{7,5},{8,10},{9,11},{10,... | collective-permute-start | bytes 442376 | tf_op jit(solution)/shard_map/ppermute | solution.py:518
  24.5 18.9 %collective-permute-start.8 = (bf16[4,8,128,128]{3,2,1,0:T(8,128)(2,1)S(1)}, bf16[4,8,128,128]{3,2,1,0:T(8,128)(2,1)S(1)}, u32[]{:S(2)}, u32[]{:S(2)}) collective-permute-start(bf16[4,8,128,128]{3,2,1,0:T(8,128)(2,1)S(1)} %get-tuple-element.55), channel_id=1, source_target_pairs={{0,1},{1,0},{2,3},{3,2},{4,5},{5,4},{6,7},{7,6},{8,9},{9,8},{10,11... | collective-permute-start | bytes 3145736 | tf_op jit(solution)/shard_map/ppermute | solution.py:562
  24.6 20.0 %collective-permute-start.3 = (bf16[4,576,128]{2,1,0:T(8,128)(2,1)S(1)}, bf16[4,576,128]{2,1,0:T(8,128)(2,1)S(1)}, u32[]{:S(2)}, u32[]{:S(2)}) collective-permute-start(bf16[4,576,128]{2,1,0:T(8,128)(2,1)S(1)} %get-tuple-element.52), channel_id=1, source_target_pairs={{0,2},{1,3},{2,0},{3,1},{4,6},{5,7},{6,4},{7,5},{8,10},{9,11},{10,... | collective-permute-start | bytes 1769480 | tf_op jit(solution)/shard_map/ppermute | solution.py:561
  26.4 1.2 %collective-permute-start.4 = (f32[2,8,128]{2,1,0:T(8,128)S(1)}, f32[2,8,128]{2,1,0:T(8,128)S(1)}, u32[]{:S(2)}, u32[]{:S(2)}) collective-permute-start(f32[2,8,128]{2,1,0:T(8,128)S(1)} %get-tuple-element.53.own_ref), channel_id=1, source_target_pairs={{0,1},{1,0},{2,3},{3,2},{4,5},{5,4},{6,7},{7,6},{8,9},{9,8},{10,11... | collective-permute-start | bytes 24584 | tf_op jit(solution)/shard_map/ppermute | solution.py:563
  28.1 6.7 %collective-permute-start.5 = (f32[2,16,128]{2,1,0:T(8,128)S(1)}, f32[2,16,128]{2,1,0:T(8,128)S(1)}, u32[]{:S(2)}, u32[]{:S(2)}) collective-permute-start(f32[2,16,128]{2,1,0:T(8,128)S(1)} %join.1.x_ref), channel_id=1, source_target_pairs={{0,4},{4,0},{8,12},{12,8},{16,20},{20,16},{24,28},{28,24},{1,5},{5... | collective-permute-start | bytes 49160 | tf_op jit(solution)/shard_map/ppermute | solution.py:575
  34.8 3.9 %collective-permute-start.6 = (f32[2,16,128]{2,1,0:T(8,128)S(1)}, f32[2,16,128]{2,1,0:T(8,128)S(1)}, u32[]{:S(2)}, u32[]{:S(2)}) collective-permute-start(f32[2,16,128]{2,1,0:T(8,128)S(1)} %add.7.x_ref), channel_id=1, source_target_pairs={{0,8},{4,12},{8,0},{12,4},{16,24},{20,28},{24,16},{28,20},{1,9},{5... | collective-permute-start | bytes 49160 | tf_op jit(solution)/shard_map/ppermute | solution.py:575
  38.8 4.6 %collective-permute-start.7 = (f32[2,16,128]{2,1,0:T(8,128)S(1)}, f32[2,16,128]{2,1,0:T(8,128)S(1)}, u32[]{:S(2)}, u32[]{:S(2)}) collective-permute-start(f32[2,16,128]{2,1,0:T(8,128)S(1)} %add.8.x_ref), channel_id=1, source_target_pairs={{0,16},{4,20},{8,24},{12,28},{16,0},{20,4},{24,8},{28,12},{1,17},{... | collective-permute-start | bytes 49160 | tf_op jit(solution)/shard_map/ppermute | solution.py:575
  43.4 5.7 %copy-start = (bf16[128,2048]{1,0:T(8,128)(2,1)S(1)}, bf16[128,2048]{1,0:T(8,128)(2,1)}, u32[]{:S(2)}) copy-start(bf16[128,2048]{1,0:T(8,128)(2,1)} %q_ref.1) | copy-start | bytes 1572868
  43.4 5.7 %copy-start.1 = (bf16[128,2048]{1,0:T(8,128)(2,1)S(1)}, bf16[128,2048]{1,0:T(8,128)(2,1)}, u32[]{:S(2)}) copy-start(bf16[128,2048]{1,0:T(8,128)(2,1)} %k_ref.1) | copy-start | bytes 1572868
  44.6 4.5 %collective-permute-start.9 = (bf16[4,576,128]{2,1,0:T(8,128)(2,1)S(1)}, bf16[4,576,128]{2,1,0:T(8,128)(2,1)S(1)}, u32[]{:S(2)}, u32[]{:S(2)}) collective-permute-start(bf16[4,576,128]{2,1,0:T(8,128)(2,1)S(1)} %collective-permute-done.3.back_ref), channel_id=1, source_target_pairs={{0,1},{1,0},{2,3},{3,2},{4,5},{5,4},{6,7},{7,6},{8,9},{9,8},{10,11... | collective-permute-start | bytes 1769480 | tf_op jit(solution)/shard_map/ppermute | solution.py:596
  44.7 3.8 %collective-permute-start.10 = (f32[2,16,128]{2,1,0:T(8,128)S(1)}, f32[2,16,128]{2,1,0:T(8,128)S(1)}, u32[]{:S(2)}, u32[]{:S(2)}) collective-permute-start(f32[2,16,128]{2,1,0:T(8,128)S(1)} %add.9), channel_id=1, source_target_pairs={{0,2},{1,3},{2,0},{3,1},{4,6},{5,7},{6,4},{7,5},{8,10},{9,11},{10,... | collective-permute-start | bytes 49160 | tf_op jit(solution)/shard_map/ppermute | solution.py:597

commit v2 on v1

v2 whole, which is shorter than its diff:
```python
import functools

import jax
import jax.numpy as jnp
from jax import lax
from jax.experimental import pallas as pl
from jax.experimental.pallas import tpu as pltpu
from jax.sharding import PartitionSpec as P


D_HEAD = 128
UNIT = 16
CORES = 2
EPSILON = 1e-06
NEG = -1e30
LOCAL_GROUP = 4
CROSS_GROUP = 2
PARTS = (2, 3)


def normalize(raw_rows, gain_vec):
    raw_f32 = raw_rows.astype(jnp.float32)
    inv_rms = lax.rsqrt(jnp.mean(raw_f32 * raw_f32, axis=-1, keepdims=True) + EPSILON)
    return ((raw_f32 * inv_rms * gain_vec).astype(jnp.bfloat16), inv_rms)


def norm_back(raw_rows, inv_rms, gain_vec, grad_norm):
    raw_f32 = raw_rows.astype(jnp.float32)
    grad_f32 = grad_norm.astype(jnp.float32)
    scaled_grad = gain_vec * grad_f32
    mean_term = jnp.mean(scaled_grad * raw_f32, axis=-1, keepdims=True)
    grad_raw = inv_rms * scaled_grad - raw_f32 * inv_rms**3 * mean_term
    return (grad_raw.astype(jnp.bfloat16), jnp.sum(grad_f32 * raw_f32 * inv_rms, axis=0))


def attend(q_norm, k_norm, val_rows, grad_rows, seg_row, vis_row):
    seq_rows, feature_count = q_norm.shape
    heads = feature_count // D_HEAD
    scale = D_HEAD ** (-0.5)
    positions = jnp.arange(seq_rows, dtype=jnp.int32)
    allowed = (seg_row[:, None] == seg_row[None, :]) & (
        (vis_row[None, :] == 1) | (positions[:, None] == positions[None, :])
    )
    f32 = jnp.float32
    q, k, v, g = (
        x.reshape(seq_rows, heads, D_HEAD) for x in (q_norm, k_norm, val_rows, grad_rows)
    )
    scores = jnp.einsum("shd,thd->hst", q, k, preferred_element_type=f32) * scale
    scores = jnp.where(allowed[None], scores, NEG)
    weights = jnp.exp(scores - jnp.max(scores, axis=-1, keepdims=True))
    prob = weights / jnp.sum(weights, axis=-1, keepdims=True)
    half = prob.astype(jnp.bfloat16)
    out = jnp.einsum("hst,thd->shd", half, v, preferred_element_type=f32)
    dprob = jnp.einsum("shd,thd->hst", g, v, preferred_element_type=f32)
    v_grad = jnp.einsum("hst,shd->thd", half, g, preferred_element_type=f32)
    row_dot = jnp.sum(prob * dprob, axis=-1, keepdims=True)
    score_grad = (prob * (dprob - row_dot) * scale).astype(jnp.bfloat16)
    q_grad = jnp.einsum("hst,thd->shd", score_grad, k, preferred_element_type=f32)
    k_grad = jnp.einsum("hst,shd->thd", score_grad, q, preferred_element_type=f32)
    return tuple(
        x.reshape(seq_rows, feature_count).astype(jnp.bfloat16)
        for x in (out, q_grad, k_grad, v_grad)
    )


def per_device_any(queries, keys, values, q_gain, k_gain, out_grad, segments, visible):
    q_norm, q_inv = normalize(queries, q_gain)
    k_norm, k_inv = normalize(keys, k_gain)
    gather = functools.partial(
        lax.all_to_all, axis_name="seq", split_axis=1, concat_axis=0, tiled=True
    )
    spread = functools.partial(
        lax.all_to_all, axis_name="seq", split_axis=0, concat_axis=1, tiled=True
    )
    parts = attend(
        *(gather(x) for x in (q_norm, k_norm, values, out_grad)), segments[0], visible[0]
    )
    attn_out, q_grad, k_grad, value_grad = (spread(x) for x in parts)
    query_grad, q_gain_part = norm_back(queries, q_inv, q_gain, q_grad)
    key_grad, k_gain_part = norm_back(keys, k_inv, k_gain, k_grad)
    q_gain_grad, k_gain_grad = lax.psum((q_gain_part, k_gain_part), ("dp", "seq"))
    return (attn_out, query_grad, key_grad, value_grad, q_gain_grad, k_gain_grad)


def units_needed(blocks, heads):
    worst = 0
    for ka in range(1, blocks + 1):
        for kb in range(1, blocks + 2 - ka):
            worst = max(worst, min(max(ka * (heads - h), kb * h) for h in range(heads + 1)))
    return worst


def dot(x, y, dims):
    return lax.dot_general(x, y, (dims, ((), ())), preferred_element_type=jnp.float32)


NT = ((1,), (1,))
NN = ((1,), (0,))
TN = ((0,), (0,))
LOG2_E = 1.4426950408889634


def attention(q, k, v, g, bias):
    scale = D_HEAD ** (-0.5)
    scores = dot(k, q, NT) * (scale * LOG2_E) + bias
    weights = jnp.exp2(scores - jnp.max(scores, axis=0, keepdims=True))
    prob = weights * (1.0 / jnp.sum(weights, axis=0, keepdims=True))
    half = prob.astype(jnp.bfloat16)
    out = dot(half, v, TN)
    dprob = dot(v, g, NT)
    v_grad = dot(half, g, NN)
    row_dot = jnp.sum(prob * dprob, axis=0, keepdims=True)
    score_grad = (prob * scale * (dprob - row_dot)).astype(jnp.bfloat16)
    q_grad = dot(score_grad, k, TN)
    k_grad = dot(score_grad, q, NN)
    return tuple(x.astype(jnp.bfloat16) for x in (out, q_grad, k_grad, v_grad))


def own_side(plan):
    first = plan[0] == 0
    heads = plan[8]
    j0 = jnp.where(first, plan[6], 0)
    j1 = jnp.where(first, heads, plan[6])
    k_own = jnp.where(first, plan[4], plan[5])
    row0 = jnp.where(first, plan[9] - UNIT * plan[4], 0)
    return j0, j1, k_own, row0


def fetch_kernel(heads, budget, q_hbm, k_hbm, v_hbm, g_hbm, seg_hbm, mine_ref, theirs_ref,
                 q_ref, k_ref, plan_ref, seg_ref, sems, head_sems):
    core = lax.rem(lax.axis_index("seq"), CORES)

    def fetch(source, target, sem):
        copy = pltpu.make_async_copy(source, target, sem)
        copy.start()
        return copy

    seg_copy = fetch(seg_hbm, seg_ref, sems.at[0])
    copies = []
    for half, target in ((1 - core, theirs_ref), (core, mine_ref)):
        for n, source in enumerate((v_hbm, g_hbm)):
            for j in range(heads):
                col = pl.ds(pl.multiple_of((half * heads + j) * D_HEAD, D_HEAD), D_HEAD)
                copies.append(fetch(source.at[:, col], target.at[n, j], head_sems.at[len(copies)]))
    copies.append(fetch(q_hbm, q_ref, sems.at[1]))
    copies.append(fetch(k_hbm, k_ref, sems.at[2]))

    seg_copy.wait()
    seg = seg_ref[...].astype(jnp.float32)
    chip_rows = seg.shape[1] // 2
    at = lax.broadcasted_iota(jnp.int32, seg.shape, 1)
    edge = jnp.sum(jnp.where(at == chip_rows - 1, seg, 0.0))
    beyond = jnp.sum(jnp.where(at == chip_rows, seg, 0.0))
    crosses = edge == beyond
    same = seg == edge
    a = jnp.sum(jnp.where(same & (at < chip_rows), 1.0, 0.0)).astype(jnp.int32)
    b = jnp.sum(jnp.where(same & (at >= chip_rows), 1.0, 0.0)).astype(jnp.int32)
    a = jnp.where(crosses, a, 0)
    b = jnp.where(crosses, b, 0)
    ka = lax.div(a + UNIT - 1, UNIT)
    kb = lax.div(b + UNIT - 1, UNIT)
    least = jnp.int32(0)
    most = jnp.int32(0)
    for h in range(heads):
        least += (ka * (heads - h) > budget).astype(jnp.int32)
        most += (kb * (h + 1) <= budget).astype(jnp.int32)
    plan_ref[0] = lax.div(lax.axis_index("seq"), CORES)
    plan_ref[1] = core
    plan_ref[2] = a
    plan_ref[3] = b
    plan_ref[4] = ka
    plan_ref[5] = kb
    plan_ref[6] = jnp.minimum(jnp.maximum(heads // 2, least), most)
    plan_ref[7] = crosses.astype(jnp.int32)
    plan_ref[8] = jnp.int32(heads)
    plan_ref[9] = jnp.int32(chip_rows)

    for copy in copies:
        copy.wait()


def prepare_kernel(rows, heads, plan, q_ref, k_ref, qg_ref, kg_ref, mine_ref, theirs_ref, inv_ref):
    for n, (raw_ref, gain_ref) in enumerate(((q_ref, qg_ref), (k_ref, kg_ref))):
        raw = raw_ref[...].astype(jnp.float32)
        inv = lax.rsqrt(jnp.mean(raw * raw, axis=-1, keepdims=True) + EPSILON)
        inv_ref[n] = jnp.broadcast_to(inv, (rows, D_HEAD))
        normed = (raw * inv * gain_ref[...]).astype(jnp.bfloat16)
        pieces = [normed[:, j * D_HEAD : (j + 1) * D_HEAD] for j in range(2 * heads)]

        @pl.when(plan[1] == 0)
        def _():
            for j in range(heads):
                mine_ref[n, j] = pieces[j]
                theirs_ref[n, j] = pieces[heads + j]

        @pl.when(plan[1] == 1)
        def _():
            for j in range(heads):
                mine_ref[n, j] = pieces[heads + j]
                theirs_ref[n, j] = pieces[j]


def pack_kernel(rows, plan, mine_ref, got_ref, *send_refs):
    core = plan[1]
    j0, j1, k_own, row0 = own_side(plan)
    for ref, half in ((mine_ref, core), (got_ref, 1 - core)):
        base = half * rows
        low = jnp.clip(lax.div(base - row0, UNIT), 0, k_own)
        high = jnp.clip(lax.div(base + rows - row0, UNIT), 0, k_own)

        def one_head(j, _, ref=ref, base=base, low=low, high=high):
            start = (j - j0) * k_own

            def unit_into(send_ref, shift):
                def one_unit(i, _):
                    at = pl.multiple_of(row0 + UNIT * i - base, UNIT)
                    to = pl.multiple_of((start + i - shift) * UNIT, UNIT)
                    for n in range(2):
                        send_ref[n, pl.ds(to, UNIT), :] = ref[n, j, pl.ds(at, UNIT), :]
                    return 0

                return one_unit

            shift, done = 0, low
            for n, send_ref in enumerate(send_refs):
                units = send_ref.shape[1] // UNIT
                last = n == len(send_refs) - 1
                cut = high if last else jnp.clip(shift + units - start, low, high)
                lax.fori_loop(done, cut, unit_into(send_ref, shift), 0)
                shift, done = shift + units, cut
            return 0

        lax.fori_loop(j0, j1, one_head, 0)


def local_kernel(rows, heads, group, plan, mine_qk, mine_vg, got_qk, got_vg, seg_ref, vis_ref, qg_ref, kg_ref,
                 keep_ref, give_ref, gain_ref, cross_bias_ref, place_ref, bias_ref, ok_ref):
    both = 2 * rows
    core, first = plan[1], plan[0] * both
    mine = [mine_qk.at[0], mine_qk.at[1], mine_vg.at[0], mine_vg.at[1]]
    got = [got_qk.at[0], got_qk.at[1], got_vg.at[0], got_vg.at[1]]

    def chip_row(ref):
        wide = ref[...].astype(jnp.float32)
        total = wide.shape[1]
        wide = jnp.broadcast_to(wide, (8, total))
        own = pltpu.roll(wide, lax.rem(2 * total - first - core * rows, total), 1)
        other = pltpu.roll(wide, lax.rem(2 * total - first - (1 - core) * rows, total), 1)
        return jnp.concatenate([own[:, :rows], other[:, :rows]], axis=1)[0:1]

    seg = jnp.broadcast_to(chip_row(seg_ref), (both, both))
    code = jnp.broadcast_to(chip_row(seg_ref) * 2.0 + chip_row(vis_ref), (both, both))
    code_t = jnp.transpose(code)
    i = lax.broadcasted_iota(jnp.int32, (both, both), 0)
    j = lax.broadcasted_iota(jnp.int32, (both, both), 1)
    gap = code_t - 2.0 * seg
    allowed = (gap == 1.0) | (i == j)
    bias_ref[...] = jnp.where(allowed, 0.0, NEG)
    r = lax.broadcasted_iota(jnp.int32, (both, D_HEAD), 0)
    at = jnp.where(r < rows, core * rows + r, (1 - core) * rows + r - rows) + first
    edge = plan[9]
    crossing = (at >= edge - plan[2]) & (at < edge + plan[3])
    ok_ref[...] = jnp.where(crossing, 0.0, 1.0)
    wide = jnp.broadcast_to(vis_ref[...].astype(jnp.float32), (8, 2 * both))
    in_first, in_last = j >= both - plan[2], j < plan[3]
    vis = jnp.where(in_first[:8], wide[:, :both], wide[:, both:])
    vis = jnp.broadcast_to(vis[0:1], (both, both)) > 0.5
    in_clip = (in_first | in_last) & ((i >= both - plan[2]) | (i < plan[3]))
    allowed = jnp.transpose(jnp.where(in_clip & vis, 1.0, 0.0)) > 0.5
    cross_bias_ref[...] = jnp.where(allowed | (i == j), 0.0, NEG)
    low, high = r < plan[3], r >= both - plan[2]
    is_first = (r >= 0) & (plan[0] == 0)
    from_own = jnp.where(is_first, jnp.where(high, 1.0, 0.0), jnp.where(low, 1.0, 0.0))
    from_far = jnp.where(is_first, jnp.where(low, 1.0, 0.0), jnp.where(high, 1.0, 0.0))
    place_ref[0] = from_own.astype(jnp.bfloat16)
    place_ref[1] = from_far.astype(jnp.bfloat16)

    def some_heads(step, _):
        for h in range(group):
            j = step * group + h
            q, k, v, g = (
                jnp.concatenate([mine[n][j], got[n][j]], axis=0) for n in range(4)
            )
            results = attention(q, k, v, g, bias_ref[...])
            for n, x in enumerate(results):
                keep_ref[n, j] = x[:rows]
                give_ref[n, j] = x[rows:]
            col = pl.ds(pl.multiple_of((core * heads + j) * D_HEAD, D_HEAD), D_HEAD)
            ok = ok_ref[...]
            for n, (x, y, gain) in enumerate(
                ((q, results[1], qg_ref), (k, results[2], kg_ref))
            ):
                term = ok * x.astype(jnp.float32) * y.astype(jnp.float32)
                gain_ref[n, pl.ds(j, 1), :] = jnp.sum(term, axis=0, keepdims=True) / gain[:, col]
        return 0

    lax.fori_loop(0, heads // group, some_heads, 0)


def crossing_kernel(rows, heads, stage, stages, group, plan, mine_refs, got_refs, far_vg, far_refs, bias_ref,
                    place_ref, qg_ref, kg_ref, gain_in, keep_ref, give_ref, gain_ref, wide_back_ref,
                    back_refs, far_ref, res_ref):
    both = 2 * rows
    core, first = plan[1], plan[0] == 0
    k_far = jnp.where(first, plan[5], plan[4])
    j0 = jnp.where(first, 0, plan[6])
    count = jnp.where(plan[7] == 1, jnp.where(first, plan[6], heads - plan[6]), 0)
    units = [ref.shape[1] // UNIT for ref in far_refs]
    ready = lambda n: jnp.minimum(lax.div(n, jnp.maximum(k_far, 1)), count)
    low = ready(sum(units[:-1])) if stage else 0
    high = ready(sum(units)) if stage < stages - 1 else count

    @pl.when(high > low)
    def _():
        at = both
        for ref in far_refs:
            far_ref[0:2, pl.ds(at, ref.shape[1]), :] = ref[...]
            at += ref.shape[1]
        far_ref[2:4, pl.ds(both, far_vg.shape[1]), :] = far_vg[...]

    gain_ref[...] = gain_in[...]
    far_lo = jnp.where(first, both, UNIT * k_far)
    res_lo = pl.multiple_of(jnp.where(first, 0, both - UNIT * k_far), UNIT)

    def some_heads(jj_first, group):
        places = [jj_first + s for s in range(group)]
        from_own, from_far = place_ref[0] > 0.5, place_ref[1] > 0.5
        for s, jj in enumerate(places):
            j = j0 + jj
            far = pl.ds(pl.multiple_of(far_lo + UNIT * jj * k_far, UNIT), both)
            loaded = []
            for n in range(4):
                mine, got = mine_refs[n // 2][n % 2, j], got_refs[n // 2][n % 2, j]
                own = jnp.where(
                    core == 0,
                    jnp.concatenate([mine, got], axis=0),
                    jnp.concatenate([got, mine], axis=0),
                )
                distant = jnp.where(from_far, far_ref[n, far, :], jnp.zeros_like(own))
                loaded.append(jnp.where(from_own, own, distant))
            q, k, v, g = loaded
            results = attention(q, k, v, g, bias_ref[...])
            own_rows = pl.ds(pl.multiple_of(core * rows, rows), rows)
            got_rows = pl.ds(pl.multiple_of((1 - core) * rows, rows), rows)
            for n, x in enumerate(results):
                res_ref[s, n, pl.ds(0, both), :] = x
            for here, ref in ((own_rows, keep_ref), (got_rows, give_ref)):
                ours = place_ref[0, here, :] > 0.5
                for n in range(4):
                    ref[n, j] = jnp.where(ours, res_ref[s, n, here, :], ref[n, j])
            col = pl.ds(pl.multiple_of((core * heads + j) * D_HEAD, D_HEAD), D_HEAD)
            for n, (x, y, gain) in enumerate(
                ((q, results[1], qg_ref), (k, results[2], kg_ref))
            ):
                term = x.astype(jnp.float32) * y.astype(jnp.float32)
                gain_ref[n, pl.ds(j, 1), :] = (
                    gain_in[n, pl.ds(j, 1), :] + jnp.sum(term, axis=0, keepdims=True) / gain[:, col]
                )
        for s, jj in enumerate(places):
            to = pl.ds(pl.multiple_of(UNIT * jj * k_far, UNIT), both)
            for n in range(4):
                wide_back_ref[n, to, :] = res_ref[s, n, pl.ds(res_lo, both), :]

    def full_group(step, _):
        some_heads(low + step * group, group)
        return 0

    def one_more(jj, _):
        some_heads(jj, 1)
        return 0

    groups = lax.div(high - low, group)
    lax.fori_loop(0, groups, full_group, 0)
    lax.fori_loop(low + groups * group, high, one_more, 0)
    at = 0
    for ref in back_refs:
        ref[...] = wide_back_ref[:, pl.ds(at, ref.shape[1]), :]
        at += ref.shape[1]


def assemble_kernel(heads, plan, keep_ref, got_ref, *to_refs):
    core = plan[1]
    for ref, side in ((keep_ref, core), (got_ref, 1 - core)):
        for j in range(heads):
            col = pl.multiple_of((side * heads + j) * D_HEAD, D_HEAD)
            for n in range(4):
                to_refs[n][:, pl.ds(col, D_HEAD)] = ref[n, j]


def join_kernel(heads, plan, own_ref, got_ref, to_ref):
    to_ref[:, pl.ds(pl.multiple_of(plan[1] * heads, heads), heads), :] = own_ref[...]
    to_ref[:, pl.ds(pl.multiple_of((1 - plan[1]) * heads, heads), heads), :] = got_ref[...]


def add_kernel(x_ref, y_ref, to_ref):
    to_ref[...] = x_ref[...] + y_ref[...]


def finish_kernel(rows, heads, pieces, plan, q_ref, k_ref, qg_ref, kg_ref, inv_ref, total_ref,
                  total_got_ref, *rest):
    backs, backs_got, rest = rest[:pieces], rest[pieces : 2 * pieces], rest[2 * pieces :]
    out_hbm, dq_hbm, dk_hbm, dv_hbm, qg_hbm, kg_hbm, *held = rest[4:14]
    wide_ref, dq_ref, dk_ref, sum_ref, sems = rest[14:]
    core = plan[1]
    j0, j1, k_own, row0 = own_side(plan)
    base = core * rows
    sum_ref[...] = total_ref[...] + total_got_ref[...]
    sums = [
        pltpu.make_async_copy(sum_ref.at[0], qg_hbm, sems.at[4]),
        pltpu.make_async_copy(sum_ref.at[1], kg_hbm, sems.at[5]),
    ]
    for copy in sums:
        copy.start()
    for s, refs in enumerate((backs, backs_got)):
        length = 0
        for ref in refs:
            wide_ref[s, :, pl.ds(rows + length, ref.shape[1]), :] = ref[...]
            length += ref.shape[1]
    r = lax.broadcasted_iota(jnp.int32, (rows, D_HEAD), 0) + base
    first = plan[0] == 0
    inside = (r >= jnp.where(first, plan[9] - plan[2], 0)) & (
        r < jnp.where(first, plan[9], plan[3])
    )

    def one_head(j, _):
        at = (j - j0) * k_own * UNIT + base - row0 + rows
        at = pl.multiple_of(jnp.clip(at, 0, length + rows), UNIT)
        for s, side in ((0, core), (1, 1 - core)):
            col = pl.multiple_of((side * heads + j) * D_HEAD, D_HEAD)
            for n in range(4):
                new = wide_ref[s, n, pl.ds(at, rows), :].astype(jnp.float32)
                old = held[n][:, pl.ds(col, D_HEAD)].astype(jnp.float32)
                held[n][:, pl.ds(col, D_HEAD)] = jnp.where(inside, new, old).astype(jnp.bfloat16)
        return 0

    lax.fori_loop(j0, jnp.where(k_own > 0, j1, j0), one_head, 0)
    copies = [
        pltpu.make_async_copy(held[0], out_hbm, sems.at[0]),
        pltpu.make_async_copy(held[3], dv_hbm, sems.at[1]),
        pltpu.make_async_copy(dq_ref, dq_hbm, sems.at[2]),
        pltpu.make_async_copy(dk_ref, dk_hbm, sems.at[3]),
    ]
    copies[0].start()
    copies[1].start()
    for n, (raw_ref, gain_ref, grad_ref, to_ref) in enumerate(
        ((q_ref, qg_ref, held[1], dq_ref), (k_ref, kg_ref, held[2], dk_ref))
    ):
        raw = raw_ref[...].astype(jnp.float32)
        scaled = gain_ref[...] * grad_ref[...].astype(jnp.float32)
        mean_term = jnp.mean(scaled * raw, axis=-1, keepdims=True)
        inv = inv_ref[n, :, 0:1]
        to_ref[...] = (inv * scaled - raw * (inv * inv * inv * mean_term)).astype(jnp.bfloat16)
        copies[2 + n].start()
    for copy in copies + sums:
        copy.wait()


def per_device_clips(queries, keys, values, q_gain, k_gain, out_grad, segments, visible, dp):
    rows, width = queries.shape
    heads = width // D_HEAD // CORES
    seq = segments.shape[1]
    budget = units_needed(CORES * rows // UNIT, heads)
    both = CORES * rows
    bf16, f32 = jnp.bfloat16, jnp.float32
    smem = pl.BlockSpec(memory_space=pltpu.SMEM)
    vmem = pl.BlockSpec(memory_space=pltpu.VMEM)
    hbm = pl.BlockSpec(memory_space=pl.ANY)
    limit = lambda mib: pltpu.CompilerParams(vmem_limit_bytes=mib << 20)
    keep_in_vmem = lambda x: pltpu.with_memory_space_constraint(x, pltpu.VMEM)
    swap_core = [(i, i ^ 1) for i in range(4)]
    swap_chip = [(i, i ^ 2) for i in range(4)]
    q_gain2, k_gain2 = q_gain[None], k_gain[None]
    split = pltpu.VMEM((4, heads, rows, D_HEAD), bf16)

    hbm_only = pl.BlockSpec(memory_space=pltpu.HBM)
    pair = pltpu.VMEM((2, heads, rows, D_HEAD), bf16)
    raw = pltpu.VMEM((rows, width), bf16)
    mine_vg, theirs_vg, raw_q, raw_k, plan = pl.pallas_call(
        functools.partial(fetch_kernel, heads, budget),
        in_specs=[hbm_only] * 5,
        out_specs=[vmem] * 4 + [smem],
        out_shape=[pair, pair, raw, raw, pltpu.SMEM((16,), jnp.int32)],
        scratch_shapes=[
            pltpu.VMEM((1, seq), jnp.int32),
            pltpu.SemaphoreType.DMA((3,)),
            pltpu.SemaphoreType.DMA((4 * heads,)),
        ],
        compiler_params=limit(4),
        name="fetch",
    )(*[pltpu.with_memory_space_constraint(x, pltpu.HBM)
        for x in (queries, keys, values, out_grad, segments)])
    got_vg = lax.ppermute(theirs_vg, "seq", swap_core)
    plan = pltpu.with_memory_space_constraint(plan, pltpu.SMEM)
    raw_q, raw_k, mine_vg, got_vg = (keep_in_vmem(x) for x in (raw_q, raw_k, mine_vg, got_vg))
    mine_qk, theirs_qk, inv = pl.pallas_call(
        functools.partial(prepare_kernel, rows, heads),
        in_specs=[smem] + [vmem] * 4,
        out_specs=[vmem] * 3,
        out_shape=[pair, pair, pltpu.VMEM((2, rows, D_HEAD), f32)],
        compiler_params=limit(8),
        name="prepare",
    )(plan, raw_q, raw_k, q_gain2, k_gain2)
    got_qk = lax.ppermute(theirs_qk, "seq", swap_core)
    mine_qk, got_qk = keep_in_vmem(mine_qk), keep_in_vmem(got_qk)

    ends = [0, *(budget * n // 4 for n in PARTS), budget]
    sizes = [y - x for x, y in zip(ends, ends[1:])]

    def pack(units, mine, got):
        return pl.pallas_call(
            functools.partial(pack_kernel, rows),
            in_specs=[smem, vmem, vmem],
            out_specs=[vmem] * len(units),
            out_shape=[pltpu.VMEM((2, n * UNIT, D_HEAD), bf16) for n in units],
            compiler_params=limit(4),
        )(plan, mine, got)

    send_vg = pack([budget], mine_vg, got_vg)[0]
    far_vg = keep_in_vmem(lax.ppermute(send_vg, "seq", swap_chip))
    fars = []
    for x in pack(sizes, mine_qk, got_qk):
        fars.append(keep_in_vmem(lax.ppermute(x, "seq", swap_chip)))

    gains_shape = pltpu.VMEM((2, heads, D_HEAD), f32)
    keep, give, gain_part, cross_bias, place = pl.pallas_call(
        functools.partial(local_kernel, rows, heads, LOCAL_GROUP),
        in_specs=[smem] + [vmem] * 8,
        out_specs=[vmem] * 5,
        out_shape=[
            split,
            split,
            gains_shape,
            pltpu.VMEM((both, both), f32),
            pltpu.VMEM((2, both, D_HEAD), bf16),
        ],
        scratch_shapes=[pltpu.VMEM((both, both), f32), pltpu.VMEM((both, D_HEAD), f32)],
        compiler_params=limit(16),
        name="local",
    )(plan, mine_qk, mine_vg, got_qk, got_vg, segments, visible, q_gain2, k_gain2)

    length = budget * UNIT
    wide_back = None
    for stage in range(len(sizes)):
        last = stage == len(sizes) - 1
        args = [plan, mine_qk, mine_vg, got_qk, got_vg, far_vg, *fars[: stage + 1]]
        args += [keep_in_vmem(cross_bias), keep_in_vmem(place), q_gain2, k_gain2]
        args += [keep_in_vmem(x) for x in (gain_part, keep, give)]
        aliases = {len(args) - 2: 0, len(args) - 1: 1}
        if stage:
            aliases[len(args)] = 3
            args.append(keep_in_vmem(wide_back))

        def body(*refs, stage=stage, count=len(args), last=last):
            ins, outs = refs[:count], list(refs[count:])
            outs[4 : 4 + last] = [outs[4 : 4 + last]]
            at = 7 + stage
            crossing_kernel(rows, heads, stage, len(sizes), CROSS_GROUP, ins[0], ins[1:3],
                            ins[3:5], ins[5], ins[6:at], *ins[at : at + 5], *outs)

        keep, give, gain_part, wide_back, *backs = pl.pallas_call(
            body,
            in_specs=[smem] + [vmem] * (len(args) - 1),
            out_specs=[vmem] * (4 + last),
            out_shape=[split, split, gains_shape, pltpu.VMEM((4, length + both, D_HEAD), bf16)]
            + [pltpu.VMEM((4, length, D_HEAD), bf16)] * last,
            input_output_aliases=aliases,
            scratch_shapes=[
                pltpu.VMEM((4, length + 2 * both, D_HEAD), bf16),
                pltpu.VMEM((CROSS_GROUP, 4, 2 * both, D_HEAD), bf16),
            ],
            compiler_params=limit(20),
        )(*args)

    gain_far = lax.ppermute(gain_part, "seq", swap_chip)
    backs = [lax.ppermute(x, "seq", swap_chip) for x in backs]
    res_got = keep_in_vmem(lax.ppermute(give, "seq", swap_core))
    add = lambda x, y: pl.pallas_call(
        add_kernel,
        in_specs=[vmem, vmem],
        out_specs=vmem,
        out_shape=pltpu.VMEM(x.shape, f32),
        compiler_params=limit(1),
        name="add",
    )(keep_in_vmem(x), keep_in_vmem(y))
    gain_part = add(gain_part, gain_far)
    gain_got = lax.ppermute(gain_part, "seq", swap_core)
    total = pl.pallas_call(
        functools.partial(join_kernel, heads),
        in_specs=[smem, vmem, vmem],
        out_specs=vmem,
        out_shape=pltpu.VMEM((2, CORES * heads, D_HEAD), f32),
        compiler_params=limit(1),
        name="join",
    )(plan, keep_in_vmem(gain_part), keep_in_vmem(gain_got))
    step = 1
    while step < dp:
        total_got = lax.ppermute(total, "dp", [(i, i ^ step) for i in range(dp)])
        step = 2 * step
        if step < dp:
            total = add(total, total_got)

    held = pl.pallas_call(
        functools.partial(assemble_kernel, heads),
        in_specs=[smem, vmem, vmem],
        out_specs=[vmem] * 4,
        out_shape=[pltpu.VMEM((rows, width), bf16)] * 4,
        compiler_params=limit(4),
        name="assemble",
    )(plan, keep_in_vmem(keep), res_got)

    backs[-1], total, held = lax.optimization_barrier((backs[-1], total, held))
    backs_got = []
    for x in backs:
        backs_got.append(keep_in_vmem(lax.ppermute(x, "seq", swap_core)))
    backs = [keep_in_vmem(x) for x in backs]

    full = jax.ShapeDtypeStruct((rows, width), bf16)
    args = [plan, raw_q, raw_k, q_gain2, k_gain2, keep_in_vmem(inv)]
    args += [keep_in_vmem(total), keep_in_vmem(total_got), *backs, *backs_got]
    args += [keep_in_vmem(x) for x in held]
    outs = pl.pallas_call(
        functools.partial(finish_kernel, rows, heads, len(backs)),
        in_specs=[smem] + [vmem] * (len(args) - 1),
        out_specs=[hbm] * 6 + [vmem] * 4,
        out_shape=[full] * 4
        + [jax.ShapeDtypeStruct((CORES * heads, D_HEAD), f32)] * 2
        + [pltpu.VMEM((rows, width), bf16)] * 4,
        input_output_aliases={len(args) - 4 + i: 6 + i for i in range(4)},
        scratch_shapes=[
            pltpu.VMEM((2, 4, length + 2 * rows, D_HEAD), bf16),
            pltpu.VMEM((rows, width), bf16),
            pltpu.VMEM((rows, width), bf16),
            pltpu.VMEM((2, CORES * heads, D_HEAD), f32),
            pltpu.SemaphoreType.DMA((6,)),
        ],
        compiler_params=limit(12),
        name="finish",
    )(*args)
    attn_out, query_grad, key_grad, value_grad = outs[:4]
    return (attn_out, query_grad, key_grad, value_grad, *(x.reshape(width) for x in outs[4:6]))


def solution(mesh):
    dp, seq = mesh.shape["dp"], mesh.shape["seq"]
    two_chips = seq == 2 * CORES and dp > 1 and dp & (dp - 1) == 0

    def per_device(queries, keys, values, q_gain, k_gain, out_grad, segments, visible):
        args = (queries, keys, values, q_gain, k_gain, out_grad, segments, visible)
        if two_chips:
            return per_device_clips(*args, dp)
        return per_device_any(*args)

    rows = P(("dp", "seq"), None)
    return jax.shard_map(
        per_device,
        mesh=mesh,
        in_specs=(rows, rows, rows, P(), P(), rows, P("dp", None), P("dp", None)),
        out_specs=(rows, rows, rows, rows, P(), P()),
        check_vma=False,
    )
```

time: 51.5 us -> 55.7 us (1.082)
  waiting for transfers between devices: 21.3 us -> 28.5 us
  Pallas kernels: 14.3 us -> 9.7 us
  starting transfers between devices: 14.4 us -> 16.4 us
    ppermute x6 -> x9, waiting for transfers between devices: 12.2 us -> 19.7 us  [the longest x1 13.8 us: per_device_clips(): gain_far = lax.ppermute(gain_part, 'seq', swap_chip)]
    ppermute x6 -> x9, starting transfers between devices: 6.94 us -> 9.38 us  [the longest x3 3.24 us: per_device_clips(): fars.append(keep_in_vmem(lax.ppermute(x, 'seq', swap_chip)))]
    pallas_call x3 -> x5, Pallas kernels: 6.09 us -> 4.22 us  [the longest x1 2.01 us: per_device_clips(): pl.pallas_call(functools.partial(fetch_kernel, heads, budget), in_specs=[...]
    pallas_call x2 -> x3, Pallas kernels: 1.13 us -> 0.04 us  [per_device_clips(): pl.pallas_call(body, in_specs=[smem] + [vmem] * (len(args) - 1), out_spec...]
    another operation x1 -> x0, local copies, waits for them, and re-layouts: 0.61 us -> none  [per_device_clips(): total[1].reshape(width)]
  transfers between devices with their start and end apart: 11 -> 14, of which waited for: 8 -> 9; matrix products, arithmetic and copies ran while one was open for 1% -> 0% of each run, Pallas kernels for 15% -> 11%
where the time goes in v2:
time: 55.7 us; the launch traced here: 55.4 us
  waiting for transfers between devices  28.5 us (51%)
  starting transfers between devices  16.4 us (29%)
  Pallas kernels  9.7 us (17%)
  between operations  0.73 us (1%)
    ppermute x1, waiting for transfers between devices, per_device_clips(): gain_far = lax.ppermute(gain_part, 'seq', swap_chip)  13.8 us
    ppermute x3, waiting for transfers between devices, per_device_clips(): total_got = lax.ppermute(total, 'dp', [(i, i ^ step) for i in range(dp)])  7.62 us
    ppermute x3, starting transfers between devices, per_device_clips(): total_got = lax.ppermute(total, 'dp', [(i, i ^ step) for i in range(dp)])  6.92 us
    ppermute x3, waiting for transfers between devices, per_device_clips(): fars.append(keep_in_vmem(lax.ppermute(x, 'seq', swap_chip)))  5.55 us
    pallas_call x1, Pallas kernels, per_device_clips(): pl.pallas_call(functools.partial(local_kernel, rows, heads, LOCAL_GROUP),...  4.81 us
    ppermute x3, starting transfers between devices, per_device_clips(): fars.append(keep_in_vmem(lax.ppermute(x, 'seq', swap_chip)))  3.24 us
    ppermute x1, starting transfers between devices, per_device_clips(): far_vg = keep_in_vmem(lax.ppermute(send_vg, 'seq', swap_chip))  2.88 us
    pallas_call x1, Pallas kernels, per_device_clips(): pl.pallas_call(functools.partial(fetch_kernel, heads, budget), in_specs=[...  2.01 us
  transfers between devices with their start and end apart: 14, of which 9 were waited for; matrix products, arithmetic and copies ran while one was open for 0% of the time, Pallas kernels for 11%

profile of v2, /device:TPU:0, one launch (start us, length us, event | category | flops | bytes accessed | tf_op | source)
XLA Modules:
  0.0 55.4 jit_solution(5283403575317267393)
XLA Ops:
  0.6 2.0 %fetch.1 = (bf16[2,8,128,128]{3,2,1,0:T(8,128)(2,1)S(1)}, bf16[2,8,128,128]{3,2,1,0:T(8,128)(2,1)S(1)}, bf16[128,2048]{1,0:T(8,128)(2,1)S(1)}, bf16[128,2048]{1,0:T(8,128)(2,1)S(1)}, s32[16]{0:T(128)S(4)}) custom-call(bf16[128,2048]{1,0:T(8,128)(2,1)} %q_hbm.1, bf16[128,2048]{1,0:T(8,128)(2,1)} %k_hbm.1, bf16[128,2048]{1,0:T(8,128)(2,1)} %v_hbm.1, ...), custom_call_target="tpu_custom_call" | custom-call | tf_op jit(solution)/shard_map/fetch/pallas_call | solution.py:478
  2.7 0.6 %collective-permute-start.1 = (bf16[2,8,128,128]{3,2,1,0:T(8,128)(2,1)S(1)}, bf16[2,8,128,128]{3,2,1,0:T(8,128)(2,1)S(1)}, u32[]{:S(2)}, u32[]{:S(2)}) collective-permute-start(bf16[2,8,128,128]{3,2,1,0:T(8,128)(2,1)S(1)} %get-tuple-element.57), channel_id=1, source_target_pairs={{0,1},{1,0},{2,3},{3,2},{4,5},{5,4},{6,7},{7,6},{8,9},{9,8},{10,11... | collective-permute-start | bytes 1572872 | tf_op jit(solution)/shard_map/ppermute | solution.py:492
  3.4 0.5 prepare.1
  3.9 0.6 collective-permute-start
  4.4 0.3 collective-permute-done.1.got_ref.got_vg.refs_4_
  4.8 2.9 %collective-permute-start.2 = (bf16[2,576,128]{2,1,0:T(8,128)(2,1)S(1)}, bf16[2,576,128]{2,1,0:T(8,128)(2,1)S(1)}, u32[]{:S(2)}, u32[]{:S(2)}) collective-permute-start(bf16[2,576,128]{2,1,0:T(8,128)(2,1)S(1)} %shard_map.127), channel_id=1, source_target_pairs={{0,2},{1,3},{2,0},{3,1},{4,6},{5,7},{6,4},{7,5},{8,10},{9,11},{10,... | collective-permute-start | bytes 884744 | tf_op jit(solution)/shard_map/ppermute | solution.py:519
  7.7 1.2 %collective-permute-start.3 = (bf16[2,288,128]{2,1,0:T(8,128)(2,1)S(1)}, bf16[2,288,128]{2,1,0:T(8,128)(2,1)S(1)}, u32[]{:S(2)}, u32[]{:S(2)}) collective-permute-start(bf16[2,288,128]{2,1,0:T(8,128)(2,1)S(1)} %get-tuple-element.58), channel_id=1, source_target_pairs={{0,2},{1,3},{2,0},{3,1},{4,6},{5,7},{6,4},{7,5},{8,10},{9,11},{10,... | collective-permute-start | bytes 442376 | tf_op jit(solution)/shard_map/ppermute | solution.py:522
  8.9 0.9 %collective-permute-start.4 = (bf16[2,144,128]{2,1,0:T(8,128)(2,1)S(1)}, bf16[2,144,128]{2,1,0:T(8,128)(2,1)S(1)}, u32[]{:S(2)}, u32[]{:S(2)}) collective-permute-start(bf16[2,144,128]{2,1,0:T(8,128)(2,1)S(1)} %get-tuple-element.59), channel_id=1, source_target_pairs={{0,2},{1,3},{2,0},{3,1},{4,6},{5,7},{6,4},{7,5},{8,10},{9,11},{10,... | collective-permute-start | bytes 221192 | tf_op jit(solution)/shard_map/ppermute | solution.py:522
  9.7 1.1 %collective-permute-start.5 = (bf16[2,144,128]{2,1,0:T(8,128)(2,1)S(1)}, bf16[2,144,128]{2,1,0:T(8,128)(2,1)S(1)}, u32[]{:S(2)}, u32[]{:S(2)}) collective-permute-start(bf16[2,144,128]{2,1,0:T(8,128)(2,1)S(1)} %get-tuple-element.60), channel_id=1, source_target_pairs={{0,2},{1,3},{2,0},{3,1},{4,6},{5,7},{6,4},{7,5},{8,10},{9,11},{10,... | collective-permute-start | bytes 221192 | tf_op jit(solution)/shard_map/ppermute | solution.py:522
  10.9 4.8 %local.1 = (bf16[4,8,128,128]{3,2,1,0:T(8,128)(2,1)S(1)}, bf16[4,8,128,128]{3,2,1,0:T(8,128)(2,1)S(1)}, f32[2,8,128]{2,1,0:T(8,128)S(1)}, f32[256,256]{1,0:T(8,128)S(1)}, bf16[2,256,128]{2,1,0:T(8,128)(2,1)S(1)}) custom-call(s32[16]{0:T(128)S(4)} %get-tuple-element.50.plan.refs_0_, bf16[2,8,128,128]{3,2,1,0:T(8,128)(2,1)S(1)} %get-tuple-element.54.mine_ref.mine_qk.refs_1_, ...), custom_call_target="tpu_custom_call" | custom-call | tf_op jit(solution)/shard_map/local/pallas_call | solution.py:525
  15.7 2.9 %collective-permute-done.3.refs_6_ = bf16[2,288,128]{2,1,0:T(8,128)(2,1)S(1)} collective-permute-done((bf16[2,288,128]{2,1,0:T(8,128)(2,1)S(1)}, bf16[2,288,128]{2,1,0:T(8,128)(2,1)S(1)}, u32[]{:S(2)}, u32[]{:S(2)}) %collective-permute-start.3) | collective-permute-done | bytes 147488 | tf_op jit(solution)/shard_map/ppermute | solution.py:522
  18.7 1.6 %collective-permute-done.4.refs_7_ = bf16[2,144,128]{2,1,0:T(8,128)(2,1)S(1)} collective-permute-done((bf16[2,144,128]{2,1,0:T(8,128)(2,1)S(1)}, bf16[2,144,128]{2,1,0:T(8,128)(2,1)S(1)}, u32[]{:S(2)}, u32[]{:S(2)}) %collective-permute-start.4) | collective-permute-done | bytes 73760 | tf_op jit(solution)/shard_map/ppermute | solution.py:522
  20.2 1.0 %collective-permute-done.5.refs_8_ = bf16[2,144,128]{2,1,0:T(8,128)(2,1)S(1)} collective-permute-done((bf16[2,144,128]{2,1,0:T(8,128)(2,1)S(1)}, bf16[2,144,128]{2,1,0:T(8,128)(2,1)S(1)}, u32[]{:S(2)}, u32[]{:S(2)}) %collective-permute-start.5) | collective-permute-done | bytes 73760 | tf_op jit(solution)/shard_map/ppermute | solution.py:522
  21.4 1.8 %collective-permute-start.6 = (bf16[4,576,128]{2,1,0:T(8,128)(2,1)S(1)}, bf16[4,576,128]{2,1,0:T(8,128)(2,1)S(1)}, u32[]{:S(2)}, u32[]{:S(2)}) collective-permute-start(bf16[4,576,128]{2,1,0:T(8,128)(2,1)S(1)} %get-tuple-element.74), channel_id=1, source_target_pairs={{0,2},{1,3},{2,0},{3,1},{4,6},{5,7},{6,4},{7,5},{8,10},{9,11},{10,... | collective-permute-start | bytes 1769480 | tf_op jit(solution)/shard_map/ppermute | solution.py:575
  23.5 13.8 %collective-permute-done.7.y_ref = f32[2,8,128]{2,1,0:T(8,128)S(1)} collective-permute-done((f32[2,8,128]{2,1,0:T(8,128)S(1)}, f32[2,8,128]{2,1,0:T(8,128)S(1)}, u32[]{:S(2)}, u32[]{:S(2)}) %collective-permute-start.7) | collective-permute-done | bytes 8224 | tf_op jit(solution)/shard_map/ppermute | solution.py:574
  37.3 1.2 %collective-permute-done.8.got_ref = f32[2,8,128]{2,1,0:T(8,128)S(1)} collective-permute-done((f32[2,8,128]{2,1,0:T(8,128)S(1)}, f32[2,8,128]{2,1,0:T(8,128)S(1)}, u32[]{:S(2)}, u32[]{:S(2)}) %collective-permute-start.8) | collective-permute-done | bytes 8224 | tf_op jit(solution)/shard_map/ppermute | solution.py:586
  38.5 4.3 %collective-permute-start.9 = (f32[2,16,128]{2,1,0:T(8,128)S(1)}, f32[2,16,128]{2,1,0:T(8,128)S(1)}, u32[]{:S(2)}, u32[]{:S(2)}) collective-permute-start(f32[2,16,128]{2,1,0:T(8,128)S(1)} %join.1.x_ref), channel_id=1, source_target_pairs={{0,4},{4,0},{8,12},{12,8},{16,20},{20,16},{24,28},{28,24},{1,5},{5... | collective-permute-start | bytes 49160 | tf_op jit(solution)/shard_map/ppermute | solution.py:597
  42.8 1.7 %collective-permute-done.9.y_ref = f32[2,16,128]{2,1,0:T(8,128)S(1)} collective-permute-done((f32[2,16,128]{2,1,0:T(8,128)S(1)}, f32[2,16,128]{2,1,0:T(8,128)S(1)}, u32[]{:S(2)}, u32[]{:S(2)}) %collective-permute-start.9) | collective-permute-done | bytes 16416 | tf_op jit(solution)/shard_map/ppermute | solution.py:597
  44.5 2.1 %collective-permute-start.10 = (f32[2,16,128]{2,1,0:T(8,128)S(1)}, f32[2,16,128]{2,1,0:T(8,128)S(1)}, u32[]{:S(2)}, u32[]{:S(2)}) collective-permute-start(f32[2,16,128]{2,1,0:T(8,128)S(1)} %add.4.x_ref), channel_id=1, source_target_pairs={{0,8},{4,12},{8,0},{12,4},{16,24},{20,28},{24,16},{28,20},{1,9},{5... | collective-permute-start | bytes 49160 | tf_op jit(solution)/shard_map/ppermute | solution.py:597
  46.6 1.7 %collective-permute-done.10.y_ref = f32[2,16,128]{2,1,0:T(8,128)S(1)} collective-permute-done((f32[2,16,128]{2,1,0:T(8,128)S(1)}, f32[2,16,128]{2,1,0:T(8,128)S(1)}, u32[]{:S(2)}, u32[]{:S(2)}) %collective-permute-start.10) | collective-permute-done | bytes 16416 | tf_op jit(solution)/shard_map/ppermute | solution.py:597
  48.3 0.6 %assemble.1 = (bf16[128,2048]{1,0:T(8,128)(2,1)S(1)}, bf16[128,2048]{1,0:T(8,128)(2,1)S(1)}, bf16[128,2048]{1,0:T(8,128)(2,1)S(1)}, bf16[128,2048]{1,0:T(8,128)(2,1)S(1)}) custom-call(s32[16]{0:T(128)S(4)} %get-tuple-element.50.plan.refs_0_, bf16[4,8,128,128]{3,2,1,0:T(8,128)(2,1)S(1)} %get-tuple-element.76.keep_ref, ...), custom_call_target="tpu_custom_call" | custom-call | tf_op jit(solution)/shard_map/assemble/pallas_call | solution.py:602
  49.0 0.5 collective-permute-start.12
  49.6 4.2 %collective-permute-done.12.total_got_ref = f32[2,16,128]{2,1,0:T(8,128)S(1)} collective-permute-done((f32[2,16,128]{2,1,0:T(8,128)S(1)}, f32[2,16,128]{2,1,0:T(8,128)S(1)}, u32[]{:S(2)}, u32[]{:S(2)}) %collective-permute-start.12) | collective-permute-done | bytes 16416 | tf_op jit(solution)/shard_map/ppermute | solution.py:597
  53.8 1.7 %finish.1 = (bf16[128,2048]{1,0:T(8,128)(2,1)}, bf16[128,2048]{1,0:T(8,128)(2,1)}, bf16[128,2048]{1,0:T(8,128)(2,1)}, bf16[128,2048]{1,0:T(8,128)(2,1)}, f32[16,...) custom-call(s32[16]{0:T(128)S(4)} %get-tuple-element.50.plan.refs_0_, ...), custom_call_target="tpu_custom_call", output_to_operand_aliasing={{6}: (10, {}), {7}: (11, {}), {8}: (12, {}), {9}: (13, {})} | custom-call | tf_op jit(solution)/shard_map/finish/pallas_call | solution.py:621
  (26 shorter events, 0.6 us)
Async XLA Ops:
  0.6 2.6 %copy-start.1 = (f32[2048]{0:T(1024)S(1)}, f32[2048]{0:T(1024)}, u32[]{:S(2)}) copy-start(f32[2048]{0:T(1024)} %param.12) | copy-start | bytes 24580
  2.7 0.7 %copy-start = (f32[2048]{0:T(1024)S(1)}, f32[2048]{0:T(1024)}, u32[]{:S(2)}) copy-start(f32[2048]{0:T(1024)} %param.11) | copy-start | bytes 24580
  2.7 2.1 %collective-permute-start.1 = (bf16[2,8,128,128]{3,2,1,0:T(8,128)(2,1)S(1)}, bf16[2,8,128,128]{3,2,1,0:T(8,128)(2,1)S(1)}, u32[]{:S(2)}, u32[]{:S(2)}) collective-permute-start(bf16[2,8,128,128]{3,2,1,0:T(8,128)(2,1)S(1)} %get-tuple-element.57), channel_id=1, source_target_pairs={{0,1},{1,0},{2,3},{3,2},{4,5},{5,4},{6,7},{7,6},{8,9},{9,8},{10,11... | collective-permute-start | bytes 1572872 | tf_op jit(solution)/shard_map/ppermute | solution.py:492
  3.9 3.8 %collective-permute-start = (bf16[2,8,128,128]{3,2,1,0:T(8,128)(2,1)S(1)}, bf16[2,8,128,128]{3,2,1,0:T(8,128)(2,1)S(1)}, u32[]{:S(2)}, u32[]{:S(2)}) collective-permute-start(bf16[2,8,128,128]{3,2,1,0:T(8,128)(2,1)S(1)} %get-tuple-element.56), channel_id=1, source_target_pairs={{0,1},{1,0},{2,3},{3,2},{4,5},{5,4},{6,7},{7,6},{8,9},{9,8},{10,11... | collective-permute-start | bytes 1572872 | tf_op jit(solution)/shard_map/ppermute | solution.py:503
  4.8 13.9 %collective-permute-start.2 = (bf16[2,576,128]{2,1,0:T(8,128)(2,1)S(1)}, bf16[2,576,128]{2,1,0:T(8,128)(2,1)S(1)}, u32[]{:S(2)}, u32[]{:S(2)}) collective-permute-start(bf16[2,576,128]{2,1,0:T(8,128)(2,1)S(1)} %shard_map.127), channel_id=1, source_target_pairs={{0,2},{1,3},{2,0},{3,1},{4,6},{5,7},{6,4},{7,5},{8,10},{9,11},{10,... | collective-permute-start | bytes 884744 | tf_op jit(solution)/shard_map/ppermute | solution.py:519
  7.6 3.2 %copy-start.3 = (s32[1,512]{1,0:T(1,128)S(1)}, s32[1,512]{1,0:T(1,128)}, u32[]{:S(2)}) copy-start(s32[1,512]{1,0:T(1,128)} %vis_ref.1) | copy-start | bytes 6148
  7.6 3.2 %copy-start.2 = (s32[1,512]{1,0:T(1,128)S(1)}, s32[1,512]{1,0:T(1,128)}, u32[]{:S(2)}) copy-start(s32[1,512]{1,0:T(1,128)} %seg_ref.1) | copy-start | bytes 6148
  7.7 11.0 %collective-permute-start.3 = (bf16[2,288,128]{2,1,0:T(8,128)(2,1)S(1)}, bf16[2,288,128]{2,1,0:T(8,128)(2,1)S(1)}, u32[]{:S(2)}, u32[]{:S(2)}) collective-permute-start(bf16[2,288,128]{2,1,0:T(8,128)(2,1)S(1)} %get-tuple-element.58), channel_id=1, source_target_pairs={{0,2},{1,3},{2,0},{3,1},{4,6},{5,7},{6,4},{7,5},{8,10},{9,11},{10,... | collective-permute-start | bytes 442376 | tf_op jit(solution)/shard_map/ppermute | solution.py:522
  8.9 11.4 %collective-permute-start.4 = (bf16[2,144,128]{2,1,0:T(8,128)(2,1)S(1)}, bf16[2,144,128]{2,1,0:T(8,128)(2,1)S(1)}, u32[]{:S(2)}, u32[]{:S(2)}) collective-permute-start(bf16[2,144,128]{2,1,0:T(8,128)(2,1)S(1)} %get-tuple-element.59), channel_id=1, source_target_pairs={{0,2},{1,3},{2,0},{3,1},{4,6},{5,7},{6,4},{7,5},{8,10},{9,11},{10,... | collective-permute-start | bytes 221192 | tf_op jit(solution)/shard_map/ppermute | solution.py:522
  9.7 11.5 %collective-permute-start.5 = (bf16[2,144,128]{2,1,0:T(8,128)(2,1)S(1)}, bf16[2,144,128]{2,1,0:T(8,128)(2,1)S(1)}, u32[]{:S(2)}, u32[]{:S(2)}) collective-permute-start(bf16[2,144,128]{2,1,0:T(8,128)(2,1)S(1)} %get-tuple-element.60), channel_id=1, source_target_pairs={{0,2},{1,3},{2,0},{3,1},{4,6},{5,7},{6,4},{7,5},{8,10},{9,11},{10,... | collective-permute-start | bytes 221192 | tf_op jit(solution)/shard_map/ppermute | solution.py:522
  21.3 27.0 %collective-permute-start.11 = (bf16[4,8,128,128]{3,2,1,0:T(8,128)(2,1)S(1)}, bf16[4,8,128,128]{3,2,1,0:T(8,128)(2,1)S(1)}, u32[]{:S(2)}, u32[]{:S(2)}) collective-permute-start(bf16[4,8,128,128]{3,2,1,0:T(8,128)(2,1)S(1)} %get-tuple-element.77), channel_id=1, source_target_pairs={{0,1},{1,0},{2,3},{3,2},{4,5},{5,4},{6,7},{7,6},{8,9},{9,8},{10,11... | collective-permute-start | bytes 3145736 | tf_op jit(solution)/shard_map/ppermute | solution.py:576
  21.4 27.6 %collective-permute-start.6 = (bf16[4,576,128]{2,1,0:T(8,128)(2,1)S(1)}, bf16[4,576,128]{2,1,0:T(8,128)(2,1)S(1)}, u32[]{:S(2)}, u32[]{:S(2)}) collective-permute-start(bf16[4,576,128]{2,1,0:T(8,128)(2,1)S(1)} %get-tuple-element.74), channel_id=1, source_target_pairs={{0,2},{1,3},{2,0},{3,1},{4,6},{5,7},{6,4},{7,5},{8,10},{9,11},{10,... | collective-permute-start | bytes 1769480 | tf_op jit(solution)/shard_map/ppermute | solution.py:575
  23.2 14.1 %collective-permute-start.7 = (f32[2,8,128]{2,1,0:T(8,128)S(1)}, f32[2,8,128]{2,1,0:T(8,128)S(1)}, u32[]{:S(2)}, u32[]{:S(2)}) collective-permute-start(f32[2,8,128]{2,1,0:T(8,128)S(1)} %get-tuple-element.75.x_ref), channel_id=1, source_target_pairs={{0,2},{1,3},{2,0},{3,1},{4,6},{5,7},{6,4},{7,5},{8,10},{9,11},{10,... | collective-permute-start | bytes 24584 | tf_op jit(solution)/shard_map/ppermute | solution.py:574
  37.3 1.2 %collective-permute-start.8 = (f32[2,8,128]{2,1,0:T(8,128)S(1)}, f32[2,8,128]{2,1,0:T(8,128)S(1)}, u32[]{:S(2)}, u32[]{:S(2)}) collective-permute-start(f32[2,8,128]{2,1,0:T(8,128)S(1)} %add.3.own_ref), channel_id=1, source_target_pairs={{0,1},{1,0},{2,3},{3,2},{4,5},{5,4},{6,7},{7,6},{8,9},{9,8},{10,11... | collective-permute-start | bytes 24584 | tf_op jit(solution)/shard_map/ppermute | solution.py:586
  38.5 6.1 %collective-permute-start.9 = (f32[2,16,128]{2,1,0:T(8,128)S(1)}, f32[2,16,128]{2,1,0:T(8,128)S(1)}, u32[]{:S(2)}, u32[]{:S(2)}) collective-permute-start(f32[2,16,128]{2,1,0:T(8,128)S(1)} %join.1.x_ref), channel_id=1, source_target_pairs={{0,4},{4,0},{8,12},{12,8},{16,20},{20,16},{24,28},{28,24},{1,5},{5... | collective-permute-start | bytes 49160 | tf_op jit(solution)/shard_map/ppermute | solution.py:597
  44.5 3.8 %collective-permute-start.10 = (f32[2,16,128]{2,1,0:T(8,128)S(1)}, f32[2,16,128]{2,1,0:T(8,128)S(1)}, u32[]{:S(2)}, u32[]{:S(2)}) collective-permute-start(f32[2,16,128]{2,1,0:T(8,128)S(1)} %add.4.x_ref), channel_id=1, source_target_pairs={{0,8},{4,12},{8,0},{12,4},{16,24},{20,28},{24,16},{28,20},{1,9},{5... | collective-permute-start | bytes 49160 | tf_op jit(solution)/shard_map/ppermute | solution.py:597
  49.0 4.8 %collective-permute-start.13 = (bf16[4,576,128]{2,1,0:T(8,128)(2,1)S(1)}, bf16[4,576,128]{2,1,0:T(8,128)(2,1)S(1)}, u32[]{:S(2)}, u32[]{:S(2)}) collective-permute-start(bf16[4,576,128]{2,1,0:T(8,128)(2,1)S(1)} %collective-permute-done.6.rest_0_), channel_id=1, source_target_pairs={{0,1},{1,0},{2,3},{3,2},{4,5},{5,4},{6,7},{7,6},{8,9},{9,8},{10,11... | collective-permute-start | bytes 1769480 | tf_op jit(solution)/shard_map/ppermute | solution.py:614
  49.0 4.7 %collective-permute-start.12 = (f32[2,16,128]{2,1,0:T(8,128)S(1)}, f32[2,16,128]{2,1,0:T(8,128)S(1)}, u32[]{:S(2)}, u32[]{:S(2)}) collective-permute-start(f32[2,16,128]{2,1,0:T(8,128)S(1)} %add.5.total_ref), channel_id=1, source_target_pairs={{0,16},{4,20},{8,24},{12,28},{16,0},{20,4},{24,8},{28,12},{1,17},{... | collective-permute-start | bytes 49160 | tf_op jit(solution)/shard_map/ppermute | solution.py:597
